TPU v7x, 64 devices: a 2x2x8 block of a 4x4x8 slice. The times are simulated.
64 devices in a mesh: dp: 4 (over x, y), tp: 16 (over z, core).
Axes of the slice: x: 2, y: 2, z: 8, core: 2. Of those that a mesh axis runs over, the one named last changes fastest.
The devices are a block of a 4x4x8 slice.
Arguments:
- tokens: bfloat16 [4, 1024, 4096], P('dp', 'tp'), parts along dimension 0
- doc_ids: int32 [4, 1024], P('dp', 'tp'), parts along dimension 0
- norm1_gain: float32 [2, 4096], replicated
- norm1_shift: float32 [2, 4096], replicated
- qkv_weight: bfloat16 [2, 4096, 3, 16, 256], P(None, None, None, 'tp')
- out_weight: bfloat16 [2, 16, 256, 4096], P(None, 'tp')
- out_bias: float32 [2, 4096], replicated
- norm2_gain: float32 [2, 4096], replicated
- norm2_shift: float32 [2, 4096], replicated
- up_weight: bfloat16 [2, 4096, 16384], P(None, None, 'tp')
- up_bias: float32 [2, 16384], P(None, 'tp')
- down_weight: bfloat16 [2, 16384, 4096], P(None, 'tp')
- down_bias: float32 [2, 4096], replicated
Outputs:
- output: bfloat16 [4, 1024, 4096], P('dp', 'tp'), parts along dimension 0
There are 4 independent parts. A program takes and returns all parts, laid end to end along the dimension named above; an argument that names none is the same for every part.
All inputs are finite; a program needn't handle non-finite values.
Results may differ from a plain program's by a relative error of at most 0.0125964.
Values are sent between devices in bfloat16 or wider.
A program may use at most 768 MiB of HBM per device.

v0:
```python
import jax
import jax.numpy as jnp
from jax import lax
from jax.sharding import PartitionSpec as P, NamedSharding

QUERY_ROWS = 512


def layer_norm(residual, gain_vec, shift_vec):
    mean_val = jnp.mean(residual, axis=-1, keepdims=True)
    centered = residual - mean_val
    variance = jnp.mean(centered * centered, axis=-1, keepdims=True)
    return (centered * lax.rsqrt(variance + 1e-5) * gain_vec + shift_vec).astype(jnp.bfloat16)


def doc_causal_attention(queries, keys_in, values_in, all_ids):
    seq_len = queries.shape[2]
    score_scale = queries.shape[3] ** -0.5
    block_rows = min(QUERY_ROWS, seq_len)
    pieces = []
    for start_row in range(0, seq_len, block_rows):
        stop_row = start_row + block_rows
        scores = jnp.einsum("bhqe,bhke->bhqk", queries[:, :, start_row:stop_row], keys_in[:, :, :stop_row], preferred_element_type=jnp.float32) * score_scale
        query_pos = start_row + jnp.arange(block_rows)
        key_pos = jnp.arange(stop_row)
        allowed = (key_pos[None, None, :] <= query_pos[None, :, None]) & (all_ids[:, start_row:stop_row, None] == all_ids[:, None, :stop_row])
        scores = jnp.where(allowed[:, None], scores, -1e30)
        probs_blk = jax.nn.softmax(scores, axis=-1).astype(jnp.bfloat16)
        pieces.append(jnp.einsum("bhqk,bhke->bqhe", probs_blk, values_in[:, :, :stop_row], preferred_element_type=jnp.float32).astype(jnp.bfloat16))
    return jnp.concatenate(pieces, axis=1)


def scatter_sum(partial_rows, groups):
    n_batch, seq_len, model_dim = partial_rows.shape
    split_rows = partial_rows.reshape(n_batch, groups, seq_len // groups, model_dim)
    received = lax.all_to_all(split_rows, "tp", 1, 1, tiled=True)
    return jnp.sum(received, axis=1, dtype=jnp.float32)


def solution(mesh):
    groups = mesh.shape["tp"]
    row_spec = P("dp", "tp", None)
    vec_spec = P(None, None)
    in_specs = (row_spec, P("dp", "tp"), vec_spec, vec_spec, P(None, None, None, "tp", None), P(None, "tp", None, None), vec_spec, vec_spec, vec_spec, P(None, None, "tp"), P(None, "tp"), P(None, "tp", None), vec_spec)

    def device_fn(tokens, doc_ids, norm1_gain, norm1_shift, qkv_weight, out_weight, out_bias, norm2_gain, norm2_shift, up_weight, up_bias, down_weight, down_bias):
        all_ids = lax.all_gather(doc_ids, "tp", axis=1, tiled=True)
        residual = tokens.astype(jnp.float32)
        for layer_idx in range(norm1_gain.shape[0]):
            normed = layer_norm(residual, norm1_gain[layer_idx], norm1_shift[layer_idx])
            full_rows = lax.all_gather(normed, "tp", axis=1, tiled=True)
            qkv_heads = jnp.einsum("bsd,dthe->tbhse", full_rows, qkv_weight[layer_idx], preferred_element_type=jnp.float32).astype(jnp.bfloat16)
            attn_out = doc_causal_attention(qkv_heads[0], qkv_heads[1], qkv_heads[2], all_ids)
            attn_part = jnp.einsum("bshe,hed->bsd", attn_out, out_weight[layer_idx], preferred_element_type=jnp.float32).astype(jnp.bfloat16)
            residual = residual + (scatter_sum(attn_part, groups) + out_bias[layer_idx])
            normed2 = layer_norm(residual, norm2_gain[layer_idx], norm2_shift[layer_idx])
            full_rows2 = lax.all_gather(normed2, "tp", axis=1, tiled=True)
            pre_act = jnp.einsum("bsd,df->bsf", full_rows2, up_weight[layer_idx], preferred_element_type=jnp.float32) + up_bias[layer_idx]
            hidden = jax.nn.gelu(pre_act, approximate=True).astype(jnp.bfloat16)
            mlp_part = jnp.einsum("bsf,fd->bsd", hidden, down_weight[layer_idx], preferred_element_type=jnp.float32).astype(jnp.bfloat16)
            residual = residual + (scatter_sum(mlp_part, groups) + down_bias[layer_idx])
        return residual.astype(jnp.bfloat16)

    return jax.shard_map(device_fn, mesh=mesh, in_specs=in_specs, out_specs=row_spec, check_vma=False)
```

profile of v0, /device:TPU:21, one launch (start us, length us, event | category | flops | bytes accessed | tf_op | source)
XLA Modules:
  0.0 1117.4 jit_solution(1125360928098359012)
XLA Ops:
  6.6 0.9 fusion.108
  7.4 0.9 fusion.109
  8.3 1.2 convert_reduce_fusion.4
  9.5 1.3 fusion.75
  10.9 2.1 fusion.78
  13.0 0.1 all-gather.5.cloned.1.call-update
  13.0 1.2 dynamic-slice
  14.8 0.8 bitcast_dynamic-update-slice_fusion
  15.6 16.1 %all-reduce = s32[1024]{0:T(1024)S(1)} all-reduce(s32[1024]{0:T(1024)S(1)} %bitcast_dynamic-update-slice_fusion), channel_id=1, replica_groups=mesh['dp'=4,'tp'=16] {'tp'}, use_global_device_ids=true, to_apply=%add | all-reduce | flops 1024 | bytes 8192
  31.7 39.1 %all-gather.5.cloned.1.call-done = bf16[1,1024,4096]{2,1,0:T(8,128)(2,1)} async-done(((bf16[1,64,4096]{2,1,0:T(8,128)(2,1)}), bf16[1,1024,4096]{2,1,0:T(8,128)(2,1)}) %all-gather.5.cloned.1.call-update) | async-done | bytes 8388624 | tf_op jit(solution)/shard_map/all_gather | solution.py:51
  70.9 10.9 fusion.64
  81.8 0.1 slice_bitcast_fusion.17
  81.9 0.8 fusion.113
  82.7 0.5 fusion.53
  83.2 0.7 fusion.73
  83.9 0.4 fusion.114
  84.3 0.2 fusion.84
  84.5 0.4 fusion.71
  84.9 1.2 copy-done.1
  86.1 5.6 convolution_convert_fusion.1
  91.7 5.0 all-to-all-start
  96.7 0.2 all-gather.7.cloned.1.call-start
  97.1 0.0 copy-start
  97.1 189.3 %all-to-all-done = bf16[1,16,64,4096]{3,2,0,1:T(8,128)(2,1)} async-done(((bf16[1,16,64,4096]{3,2,0,1:T(8,128)(2,1)}), bf16[1,16,64,4096]{3,2,0,1:T(8,128)(2,1)}, u32[]{:S(2)}, u32[]{:S(2)}) %all-to-all-start) | async-done | bytes 8388640 | tf_op jit(solution)/shard_map/all_to_all | solution.py:36
  286.4 5.0 convert_reduce_fusion.3
  291.4 0.2 fusion.100
  291.7 0.3 multiply_reduce_fusion.2
  292.0 1.1 add_convert_fusion.2
  293.1 0.1 all-gather.7.cloned.1.call-update
  293.2 54.0 %all-gather.7.cloned.1.call-done = bf16[1,1024,4096]{2,1,0:T(8,128)(2,1)} async-done(((bf16[1,64,4096]{2,1,0:T(8,128)(2,1)}), bf16[1,1024,4096]{2,1,0:T(8,128)(2,1)}) %all-gather.7.cloned.1.call-update) | async-done | bytes 8388624 | tf_op jit(solution)/shard_map/all_gather | solution.py:57
  347.2 14.6 %fusion.31 = bf16[1024,1024]{1,0:T(8,128)(2,1)S(1)} fusion(bf16[2,4096,1024]{2,1,0:T(8,128)(2,1)} %param.22, bf16[1,1024,4096]{2,1,0:T(8,128)(2,1)} %all-gather.7.cloned.1.call-done, f32[1024]{0:T(1024)S(1)} %bitcast.250), kind=kOutput, calls=%fused_computation.37 | convolution fusion | flops 8600420352 | bytes 18878464 | tf_op jit(solution)/shard_map/bsd,df->bsf/dot_general | solution.py:58
  361.8 14.2 %fusion.18 = bf16[1024,4096]{1,0:T(8,128)(2,1)} fusion(bf16[1024,1024]{1,0:T(8,128)(2,1)S(1)} %fusion.31, bf16[2,1024,4096]{2,1,0:T(8,128)(2,1)} %param.24), kind=kOutput, calls=%fused_computation.22 | convolution fusion | flops 8594128896 | bytes 18874368 | tf_op jit(solution)/shard_map/bsf,fd->bsd/dot_general | solution.py:60
  376.0 5.0 all-to-all-start.1
  381.0 0.1 all-gather.9.cloned.1.call-start
  381.1 189.5 %all-to-all-done.1 = bf16[1,16,64,4096]{3,2,0,1:T(8,128)(2,1)} async-done(((bf16[1,16,64,4096]{3,2,0,1:T(8,128)(2,1)}), bf16[1,16,64,4096]{3,2,0,1:T(8,128)(2,1)}, u32[]{:S(2)}, u32[]{:S(2)}) %all-to-all-start.1) | async-done | bytes 8388640 | tf_op jit(solution)/shard_map/all_to_all | solution.py:36
  570.7 5.0 convert_reduce_fusion.2
  575.7 0.3 fusion.103
  576.1 0.3 multiply_reduce_fusion.1
  576.4 1.0 add_convert_fusion.1
  577.4 0.1 all-gather.9.cloned.1.call-update
  577.5 0.3 all-gather.11.cloned.1.call-start
  577.8 53.7 %all-gather.9.cloned.1.call-done = bf16[1,1024,4096]{2,1,0:T(8,128)(2,1)} async-done(((bf16[1,64,4096]{2,1,0:T(8,128)(2,1)}), bf16[1,1024,4096]{2,1,0:T(8,128)(2,1)}) %all-gather.9.cloned.1.call-update) | async-done | bytes 8388624 | tf_op jit(solution)/shard_map/all_gather | solution.py:51
  631.5 10.9 fusion.61
  642.4 0.1 slice_bitcast_fusion.15
  642.5 0.8 fusion.115
  643.3 0.4 fusion.116
  643.6 0.5 fusion.54
  644.1 0.7 fusion.74
  644.8 0.2 fusion.85
  645.0 0.4 fusion.72
  645.4 1.6 copy-done.2
  647.0 2.4 convolution_convert_fusion
  649.4 190.2 %all_to_all.20 = bf16[1,16,64,4096]{3,2,0,1:T(8,128)(2,1)S(1)} all-to-all(bf16[1,16,64,4096]{3,2,0,1:T(8,128)(2,1)S(1)} %bitcast.230), channel_id=1, replica_groups=mesh['dp'=4,'tp'=16] {'tp'}, dimensions={1} | all-to-all | bytes 16777216 | tf_op jit(solution)/shard_map/all_to_all | solution.py:36
  839.5 1.5 convert_reduce_fusion.1
  841.1 0.3 fusion.101
  841.4 0.3 multiply_reduce_fusion
  841.7 1.0 add_convert_fusion
  842.7 0.1 all-gather.11.cloned.1.call-update
  842.8 49.4 %all-gather.11.cloned.1.call-done = bf16[1,1024,4096]{2,1,0:T(8,128)(2,1)} async-done(((bf16[1,64,4096]{2,1,0:T(8,128)(2,1)}), bf16[1,1024,4096]{2,1,0:T(8,128)(2,1)}) %all-gather.11.cloned.1.call-update) | async-done | bytes 8388624 | tf_op jit(solution)/shard_map/all_gather | solution.py:57
  892.1 14.6 %fusion.39 = bf16[1024,1024]{1,0:T(8,128)(2,1)S(1)} fusion(bf16[2,4096,1024]{2,1,0:T(8,128)(2,1)} %param.22, bf16[1,1024,4096]{2,1,0:T(8,128)(2,1)} %all-gather.11.cloned.1.call-done, f32[1024]{0:T(1024)S(1)} %bitcast.249), kind=kOutput, calls=%fused_computation.45 | convolution fusion | flops 8600420352 | bytes 18878464 | tf_op jit(solution)/shard_map/bsd,df->bsf/dot_general | solution.py:58
  906.8 11.2 %fusion.21 = bf16[1024,4096]{1,0:T(8,128)(2,1)S(1)} fusion(bf16[1024,1024]{1,0:T(8,128)(2,1)S(1)} %fusion.39, bf16[2,1024,4096]{2,1,0:T(8,128)(2,1)} %param.24), kind=kOutput, calls=%fused_computation.23 | convolution fusion | flops 8594128896 | bytes 18874368 | tf_op jit(solution)/shard_map/bsf,fd->bsd/dot_general | solution.py:60
  918.0 189.9 %all_to_all.21 = bf16[1,16,64,4096]{3,2,0,1:T(8,128)(2,1)S(1)} all-to-all(bf16[1,16,64,4096]{3,2,0,1:T(8,128)(2,1)S(1)} %bitcast.232), channel_id=1, replica_groups=mesh['dp'=4,'tp'=16] {'tp'}, dimensions={1} | all-to-all | bytes 16777216 | tf_op jit(solution)/shard_map/all_to_all | solution.py:36
  1107.9 1.5 convert_reduce_fusion
  1109.5 0.9 fusion.80
  (30 shorter events, 0.2 us)
Async XLA Ops:
  6.5 64.3 %all-gather.5.cloned.1.call-start = ((), (), s32[]{:S(2)}) async-start(), calls=%async_computation.4 | async-start | bytes 8912896 | tf_op jit(solution)/shard_map/all_gather | solution.py:51
  83.9 2.2 copy-start.1
  91.7 5.3 copy-start.3
  91.7 5.3 copy-start.4
  91.7 5.3 copy-start.5
  91.7 194.7 %all-to-all-start = ((bf16[1,16,64,4096]{3,2,0,1:T(8,128)(2,1)}), bf16[1,16,64,4096]{3,2,0,1:T(8,128)(2,1)}, u32[]{:S(2)}, u32[]{:S(2)}) async-start(bf16[1,16,64,4096]{3,2,0,1:T(8,128)(2,1)} %bitcast.229), calls=%async_computation | async-start | bytes 16777216 | tf_op jit(solution)/shard_map/all_to_all | solution.py:36
  96.7 250.5 %all-gather.7.cloned.1.call-start = ((), (), s32[]{:S(2)}) async-start(), calls=%async_computation.5 | async-start | bytes 8912896 | tf_op jit(solution)/shard_map/all_gather | solution.py:57
  97.1 194.4 %copy-start = (bf16[1,64,4096]{2,1,0:T(8,128)(2,1)S(1)}, bf16[1,64,4096]{2,1,0:T(8,128)(2,1)}, u32[]{:S(2)}) copy-start(bf16[1,64,4096]{2,1,0:T(8,128)(2,1)} %param.13) | copy-start | bytes 1572868
  291.4 1.8 copy-start.7
  376.0 5.1 copy-start.6
  376.0 194.7 %all-to-all-start.1 = ((bf16[1,16,64,4096]{3,2,0,1:T(8,128)(2,1)}), bf16[1,16,64,4096]{3,2,0,1:T(8,128)(2,1)}, u32[]{:S(2)}, u32[]{:S(2)}) async-start(bf16[1,16,64,4096]{3,2,0,1:T(8,128)(2,1)} %bitcast.231), calls=%async_computation.1 | async-start | bytes 16777216 | tf_op jit(solution)/shard_map/all_to_all | solution.py:36
  381.0 250.4 %all-gather.9.cloned.1.call-start = ((), (), s32[]{:S(2)}) async-start(), calls=%async_computation.6 | async-start | bytes 8912896 | tf_op jit(solution)/shard_map/all_gather | solution.py:51
  577.5 314.7 %all-gather.11.cloned.1.call-start = ((), (), s32[]{:S(2)}) async-start(), calls=%async_computation.7 | async-start | bytes 8912896 | tf_op jit(solution)/shard_map/all_gather | solution.py:57
  644.8 2.2 copy-start.2
Sparse Core Ops, SparseCore 0:
  13.2 57.6 all-gather.4
  293.3 53.8 all-gather.6
  577.6 53.8 all-gather.8
  842.9 49.2 all-gather.10
where the time goes:
time: 1130 us; the launch traced here: 1120 us
  waiting for transfers between devices  575 us (51%)
  blocking collectives  396 us (35%)
  matrix products  88.9 us (8%)
  other arithmetic  25.1 us (2%)
  between operations  14.5 us (1%)
    all_to_all x2, blocking collectives, scatter_sum(): received = lax.all_to_all(split_rows, 'tp', 1, 1, tiled=True)  380 us
    all_to_all x2, waiting for transfers between devices, scatter_sum(): received = lax.all_to_all(split_rows, 'tp', 1, 1, tiled=True)  379 us
    all_gather x2, waiting for transfers between devices, device_fn(): full_rows2 = lax.all_gather(normed2, 'tp', axis=1, tiled=True)  103 us
    all_gather x2, waiting for transfers between devices, device_fn(): full_rows = lax.all_gather(normed, 'tp', axis=1, tiled=True)  92.8 us
    dot_general x2, matrix products, device_fn(): jnp.einsum('bsd,df->bsf', full_rows2, up_weight[layer_idx], preferred_ele...  29.2 us
    dot_general x2, matrix products, device_fn(): jnp.einsum('bsf,fd->bsd', hidden, down_weight[layer_idx], preferred_eleme...  25.5 us
  transfers between devices with their start and end apart: 6, of which 6 were waited for; matrix products, arithmetic and copies ran while one was open for 0% of the time, Pallas kernels for 0%

commit v1 on v0

--- a/solution.py
+++ b/solution.py
@@ -31,10 +31,7 @@
 
 
 def scatter_sum(partial_rows, groups):
-    n_batch, seq_len, model_dim = partial_rows.shape
-    split_rows = partial_rows.reshape(n_batch, groups, seq_len // groups, model_dim)
-    received = lax.all_to_all(split_rows, "tp", 1, 1, tiled=True)
-    return jnp.sum(received, axis=1, dtype=jnp.float32)
+    return lax.psum_scatter(partial_rows.astype(jnp.float32), "tp", scatter_dimension=1, tiled=True)
 
 
 def solution(mesh):

time: 1130 us -> 734 us (0.65); the launches traced: 1120 us -> 734 us
  blocking collectives: 396 us -> 16.1 us
  matrix products: 88.9 us -> 101 us
    all_to_all x2 -> x0, blocking collectives: 380 us -> none  [scatter_sum(): received = lax.all_to_all(split_rows, 'tp', 1, 1, tiled=True)]
    all_to_all x2 -> x0, waiting for transfers between devices: 379 us -> none  [scatter_sum(): received = lax.all_to_all(split_rows, 'tp', 1, 1, tiled=True)]
    reduce_scatter x0 -> x4, waiting for transfers between devices: none -> 378 us  [scatter_sum(): lax.psum_scatter(partial_rows.astype(jnp.float32), 'tp', scatter_dimensio...]
    reduce_sum x4 -> x0, other arithmetic: 13.2 us -> none  [scatter_sum(): return jnp.sum(received, axis=1, dtype=jnp.float32)]
  transfers between devices with their start and end apart: 6 -> 8, of which waited for: 6 -> 8; matrix products, arithmetic and copies ran while one was open for 0% -> 0% of each run, Pallas kernels for 0% -> 0%
where the time goes in v1:
time: 734 us
  waiting for transfers between devices  574 us (78%)
  matrix products  101 us (14%)
  other arithmetic  19.5 us (3%)
  blocking collectives  16.1 us (2%)
  between operations  14.4 us (2%)
  local copies, waits for them, and re-layouts  8.09 us (1%)
    reduce_scatter x4, waiting for transfers between devices, scatter_sum(): lax.psum_scatter(partial_rows.astype(jnp.float32), 'tp', scatter_dimensio...  378 us
    all_gather x2, waiting for transfers between devices, device_fn(): full_rows2 = lax.all_gather(normed2, 'tp', axis=1, tiled=True)  104 us
    all_gather x2, waiting for transfers between devices, device_fn(): full_rows = lax.all_gather(normed, 'tp', axis=1, tiled=True)  91.1 us
    dot_general x2, matrix products, device_fn(): jnp.einsum('bsd,df->bsf', full_rows2, up_weight[layer_idx], preferred_ele...  29.2 us
    dot_general x2, matrix products, device_fn(): jnp.einsum('bsf,fd->bsd', hidden, down_weight[layer_idx], preferred_eleme...  28.8 us
    dot_general x2, matrix products, device_fn(): jnp.einsum('bsd,dthe->tbhse', full_rows, qkv_weight[layer_idx], preferred...  21.8 us
    dot_general x2, matrix products, device_fn(): jnp.einsum('bshe,hed->bsd', attn_out, out_weight[layer_idx], preferred_el...  16.2 us
    unnamed x1, blocking collectives  16.1 us
  transfers between devices with their start and end apart: 8, of which 8 were waited for; matrix products, arithmetic and copies ran while one was open for 0% of the time, Pallas kernels for 0%

profile of v1, /device:TPU:21, one launch (start us, length us, event | category | flops | bytes accessed | tf_op | source)
XLA Modules:
  0.0 733.6 jit_solution(14097970710567159277)
XLA Ops:
  6.6 0.9 fusion.101
  7.4 0.9 fusion.102
  8.3 1.2 convert_reduce_fusion
  9.5 1.3 fusion.73
  10.9 2.1 fusion.76
  13.0 0.1 all-gather.5.cloned.1.call-update
  13.0 0.1 reduce-scatter.5.cloned.1.call-start
  13.1 1.2 dynamic-slice
  14.9 0.8 bitcast_dynamic-update-slice_fusion
  15.7 16.1 %all-reduce = s32[1024]{0:T(1024)S(1)} all-reduce(s32[1024]{0:T(1024)S(1)} %bitcast_dynamic-update-slice_fusion), channel_id=1, replica_groups=mesh['dp'=4,'tp'=16] {'tp'}, use_global_device_ids=true, to_apply=%add | all-reduce | flops 1024 | bytes 8192
  31.8 39.1 %all-gather.5.cloned.1.call-done = bf16[1,1024,4096]{2,1,0:T(8,128)(2,1)} async-done(((bf16[1,64,4096]{2,1,0:T(8,128)(2,1)}), bf16[1,1024,4096]{2,1,0:T(8,128)(2,1)}) %all-gather.5.cloned.1.call-update) | async-done | bytes 8388624 | tf_op jit(solution)/shard_map/all_gather | solution.py:48
  70.9 10.9 %fusion.62 = bf16[3,1,1,1024,256]{4,3,0,1,2:T(8,128)(2,1)S(1)} fusion(bf16[2,4096,3,1,256]{4,1,2,3,0:T(8,128)(2,1)} %bitcast.222, bf16[1,1024,4096]{2,1,0:T(8,128)(2,1)} %all-gather.5.cloned.1.call-done), kind=kOutput, calls=%fused_computation.62 | convolution fusion | flops 6443237376 | bytes 16252928 | tf_op jit(solution)/shard_map/bsd,dthe->tbhse/dot_general | solution.py:49
  81.8 0.1 slice_bitcast_fusion.17
  81.9 0.8 fusion.105
  82.7 0.5 fusion.51
  83.2 0.7 fusion.71
  83.9 0.4 fusion.106
  84.3 0.2 fusion.78
  84.5 0.4 fusion.69
  84.9 1.2 copy-done.2
  86.1 8.1 %bitcast_convert_fusion.3 = f32[1,1024,4096]{2,1,0:T(8,128)} fusion(bf16[2,1,256,4096]{3,2,1,0:T(8,128)(2,1)S(1)} %copy-done.2, bf16[1,512,1,256]{1,3,2,0:T(8,128)(2,1)S(1)} %fusion.71, bf16[1,512,1,256]{1,3,2,0:T(8,128)(2,1)S(1)} %fusion.69), kind=kOutput, calls=%fused_computation.3 | convolution fusion | flops 2156920832 | bytes 19398656 | tf_op jit(solution)/shard_map/bshe,hed->bsd/dot_general | solution.py:51
  94.2 0.1 reduce-scatter.5.cloned.1.call-update
  94.3 0.1 all-gather.7.cloned.1.call-start
  94.3 0.6 copy-done.4
  95.1 94.2 %reduce-scatter.5.cloned.1.call-done = f32[1,64,4096]{2,1,0:T(8,128)} async-done(((f32[1,1024,4096]{2,1,0:T(8,128)}), f32[1,64,4096]{2,1,0:T(8,128)}) %reduce-scatter.5.cloned.1.call-update) | async-done | bytes 1048592 | tf_op jit(solution)/shard_map/reduce_scatter | solution.py:34
  189.3 1.5 fusion.94
  190.7 1.6 multiply_reduce_fusion.2
  192.3 2.3 add_convert_fusion.3
  194.7 0.1 all-gather.7.cloned.1.call-update
  194.7 0.2 reduce-scatter.7.cloned.1.call-start
  195.0 52.0 %all-gather.7.cloned.1.call-done = bf16[1,1024,4096]{2,1,0:T(8,128)(2,1)} async-done(((bf16[1,64,4096]{2,1,0:T(8,128)(2,1)}), bf16[1,1024,4096]{2,1,0:T(8,128)(2,1)}) %all-gather.7.cloned.1.call-update) | async-done | bytes 8388624 | tf_op jit(solution)/shard_map/all_gather | solution.py:54
  247.0 14.6 %fusion.29 = bf16[1024,1024]{1,0:T(8,128)(2,1)S(1)} fusion(bf16[2,4096,1024]{2,1,0:T(8,128)(2,1)} %param.22, bf16[1,1024,4096]{2,1,0:T(8,128)(2,1)} %all-gather.7.cloned.1.call-done, f32[1024]{0:T(1024)S(1)} %bitcast.217), kind=kOutput, calls=%fused_computation.33 | convolution fusion | flops 8600420352 | bytes 18878464 | tf_op jit(solution)/shard_map/bsd,df->bsf/dot_general | solution.py:55
  261.7 14.4 %bitcast_convert_fusion.2 = f32[1,1024,4096]{2,1,0:T(8,128)} fusion(bf16[1024,1024]{1,0:T(8,128)(2,1)S(1)} %fusion.29, bf16[2,1024,4096]{2,1,0:T(8,128)(2,1)} %param.24), kind=kOutput, calls=%fused_computation.2 | convolution fusion | flops 8598323200 | bytes 27262976 | tf_op jit(solution)/shard_map/bsf,fd->bsd/dot_general | solution.py:57
  276.2 0.1 all-gather.9.cloned.1.call-start
  276.2 0.6 copy-done.7
  276.9 94.3 %reduce-scatter.7.cloned.1.call-done = f32[1,64,4096]{2,1,0:T(8,128)} async-done(((f32[1,1024,4096]{2,1,0:T(8,128)}), f32[1,64,4096]{2,1,0:T(8,128)}) %reduce-scatter.7.cloned.1.call-update) | async-done | bytes 1048592 | tf_op jit(solution)/shard_map/reduce_scatter | solution.py:34
  371.1 1.6 fusion.96
  372.8 0.3 multiply_reduce_fusion.1
  373.1 1.0 add_convert_fusion.2
  374.1 0.1 all-gather.9.cloned.1.call-update
  374.2 0.3 reduce-scatter.9.cloned.1.call-start
  374.5 52.0 %all-gather.9.cloned.1.call-done = bf16[1,1024,4096]{2,1,0:T(8,128)(2,1)} async-done(((bf16[1,64,4096]{2,1,0:T(8,128)(2,1)}), bf16[1,1024,4096]{2,1,0:T(8,128)(2,1)}) %all-gather.9.cloned.1.call-update) | async-done | bytes 8388624 | tf_op jit(solution)/shard_map/all_gather | solution.py:48
  426.5 10.9 %fusion.59 = bf16[3,1,1,1024,256]{4,3,0,1,2:T(8,128)(2,1)S(1)} fusion(bf16[2,4096,3,1,256]{4,1,2,3,0:T(8,128)(2,1)} %bitcast.223, bf16[1,1024,4096]{2,1,0:T(8,128)(2,1)} %all-gather.9.cloned.1.call-done), kind=kOutput, calls=%fused_computation.61 | convolution fusion | flops 6443237376 | bytes 16252928 | tf_op jit(solution)/shard_map/bsd,dthe->tbhse/dot_general | solution.py:49
  437.4 0.1 slice_bitcast_fusion.15
  437.5 0.8 fusion.107
  438.3 0.4 fusion.108
  438.7 0.5 fusion.52
  439.2 0.7 fusion.72
  439.9 0.2 fusion.79
  440.1 0.4 fusion.70
  440.5 1.6 copy-done.3
  442.1 8.1 %bitcast_convert_fusion.1 = f32[1,1024,4096]{2,1,0:T(8,128)} fusion(bf16[2,1,256,4096]{3,2,1,0:T(8,128)(2,1)S(1)} %copy-done.3, bf16[1,512,1,256]{1,3,2,0:T(8,128)(2,1)S(1)} %fusion.72, bf16[1,512,1,256]{1,3,2,0:T(8,128)(2,1)S(1)} %fusion.70), kind=kOutput, calls=%fused_computation.1 | convolution fusion | flops 2156920832 | bytes 19398656 | tf_op jit(solution)/shard_map/bshe,hed->bsd/dot_general | solution.py:51
  450.2 0.1 reduce-scatter.9.cloned.1.call-update
  450.2 0.1 all-gather.11.cloned.1.call-start
  450.3 94.9 %reduce-scatter.9.cloned.1.call-done = f32[1,64,4096]{2,1,0:T(8,128)} async-done(((f32[1,1024,4096]{2,1,0:T(8,128)}), f32[1,64,4096]{2,1,0:T(8,128)}) %reduce-scatter.9.cloned.1.call-update) | async-done | bytes 1048592 | tf_op jit(solution)/shard_map/reduce_scatter | solution.py:34
  545.2 1.5 fusion.95
  546.8 0.3 multiply_reduce_fusion
  547.1 1.0 add_convert_fusion.1
  548.2 0.3 reduce-scatter.11.cloned.1.call-start
  548.5 52.0 %all-gather.11.cloned.1.call-done = bf16[1,1024,4096]{2,1,0:T(8,128)(2,1)} async-done(((bf16[1,64,4096]{2,1,0:T(8,128)(2,1)}), bf16[1,1024,4096]{2,1,0:T(8,128)(2,1)}) %all-gather.11.cloned.1.call-update) | async-done | bytes 8388624 | tf_op jit(solution)/shard_map/all_gather | solution.py:54
  600.5 14.6 %fusion.37 = bf16[1024,1024]{1,0:T(8,128)(2,1)S(1)} fusion(bf16[2,4096,1024]{2,1,0:T(8,128)(2,1)} %param.22, bf16[1,1024,4096]{2,1,0:T(8,128)(2,1)} %all-gather.11.cloned.1.call-done, f32[1024]{0:T(1024)S(1)} %bitcast.216), kind=kOutput, calls=%fused_computation.41 | convolution fusion | flops 8600420352 | bytes 18878464 | tf_op jit(solution)/shard_map/bsd,df->bsf/dot_general | solution.py:55
  615.1 14.4 %bitcast_convert_fusion = f32[1,1024,4096]{2,1,0:T(8,128)} fusion(bf16[1024,1024]{1,0:T(8,128)(2,1)S(1)} %fusion.37, bf16[2,1024,4096]{2,1,0:T(8,128)(2,1)} %param.24), kind=kOutput, calls=%fused_computation | convolution fusion | flops 8598323200 | bytes 27262976 | tf_op jit(solution)/shard_map/bsf,fd->bsd/dot_general | solution.py:57
  629.6 95.0 %reduce-scatter.11.cloned.1.call-done = f32[1,64,4096]{2,1,0:T(8,128)} async-done(((f32[1,1024,4096]{2,1,0:T(8,128)}), f32[1,64,4096]{2,1,0:T(8,128)}) %reduce-scatter.11.cloned.1.call-update) | async-done | bytes 1048592 | tf_op jit(solution)/shard_map/reduce_scatter | solution.py:34
  724.6 2.2 add_convert_fusion
  (34 shorter events, 0.4 us)
Async XLA Ops:
  6.5 64.3 %all-gather.5.cloned.1.call-start = ((), (), s32[]{:S(2)}) async-start(), calls=%async_computation.4 | async-start | bytes 8912896 | tf_op jit(solution)/shard_map/all_gather | solution.py:48
  13.0 176.2 %reduce-scatter.5.cloned.1.call-start = ((), (), s32[]{:S(2)}) async-start(), calls=%async_computation.5 | async-start | bytes 17825792 | tf_op jit(solution)/shard_map/reduce_scatter | solution.py:34
  83.9 2.2 copy-start.2
  94.2 0.8 copy-start.4
  94.2 0.8 copy-start.5
  94.2 0.8 copy-start.6
  94.2 95.1 %copy-start = (bf16[1,64,4096]{2,1,0:T(8,128)(2,1)S(1)}, bf16[1,64,4096]{2,1,0:T(8,128)(2,1)}, u32[]{:S(2)}) copy-start(bf16[1,64,4096]{2,1,0:T(8,128)(2,1)} %param.13) | copy-start | bytes 1572868
  94.2 100.7 %copy-start.8 = (f32[2,1024]{1,0:T(2,128)S(1)}, f32[2,1024]{1,0:T(2,128)}, u32[]{:S(2)}) copy-start(f32[2,1024]{1,0:T(2,128)} %param.23) | copy-start | bytes 24580
  94.3 152.8 %all-gather.7.cloned.1.call-start = ((), (), s32[]{:S(2)}) async-start(), calls=%async_computation.6 | async-start | bytes 8912896 | tf_op jit(solution)/shard_map/all_gather | solution.py:54
  194.7 176.4 %reduce-scatter.7.cloned.1.call-start = ((), (), s32[]{:S(2)}) async-start(), calls=%async_computation.7 | async-start | bytes 17825792 | tf_op jit(solution)/shard_map/reduce_scatter | solution.py:34
  276.1 0.8 copy-start.7
  276.1 95.0 %copy-start.1 = (f32[1,64,4096]{2,1,0:T(8,128)S(1)}, f32[1,64,4096]{2,1,0:T(8,128)}, u32[]{:S(2)}) copy-start(f32[1,64,4096]{2,1,0:T(8,128)} %reduce-scatter.5.cloned.1.call-done) | copy-start | bytes 3145732
  276.2 150.3 %all-gather.9.cloned.1.call-start = ((), (), s32[]{:S(2)}) async-start(), calls=%async_computation.8 | async-start | bytes 8912896 | tf_op jit(solution)/shard_map/all_gather | solution.py:48
  374.2 171.1 %reduce-scatter.9.cloned.1.call-start = ((), (), s32[]{:S(2)}) async-start(), calls=%async_computation.9 | async-start | bytes 17825792 | tf_op jit(solution)/shard_map/reduce_scatter | solution.py:34
  439.9 2.2 copy-start.3
  450.2 150.3 %all-gather.11.cloned.1.call-start = ((), (), s32[]{:S(2)}) async-start(), calls=%async_computation.10 | async-start | bytes 8912896 | tf_op jit(solution)/shard_map/all_gather | solution.py:54
  548.2 176.4 %reduce-scatter.11.cloned.1.call-start = ((), (), s32[]{:S(2)}) async-start(), calls=%async_computation.11 | async-start | bytes 17825792 | tf_op jit(solution)/shard_map/reduce_scatter | solution.py:34
Sparse Core Ops, SparseCore 0:
  13.2 57.6 all-gather.4
  94.4 94.8 reduce-scatter.4
  194.8 52.1 all-gather.6
  276.3 94.8 reduce-scatter.6
  374.3 52.1 all-gather.8
  450.4 94.8 reduce-scatter.8
  548.3 52.1 all-gather.10
  629.7 94.8 reduce-scatter.10

commit v2 on v1

v2 whole, which is shorter than its diff:
```python
import functools

import jax
import jax.numpy as jnp
from jax import lax
from jax.experimental import pallas as pl
from jax.experimental.pallas import tpu as pltpu
from jax.sharding import PartitionSpec as P

MESH = pl.DeviceIdType.MESH
F32, BF16 = jnp.float32, jnp.bfloat16
ID_COLS = 128
RIGHT, LEFT = 0, 1


def loop(count, body):
    lax.fori_loop(0, count, lambda i, carry: (body(i), carry)[1], 0)


def cols_at(i, width):
    return pl.ds(pl.multiple_of(i * width, width), width)


def block_kernel(n, tokens_ref, ids_ref, g1_ref, s1_ref, ob_ref, g2_ref, s2_ref, ub_ref, db_ref, wqkv_hbm, wout_hbm, wup_hbm, wdown_hbm,
                 out_ref, hbuf, part, psib, ring, fresh, resid, wqkv, wout, wup, wdown, qkv, hidden, kpos, kids,
                 ag_send, ag_recv, sib_send, sib_recv, own_sem, part_send, part_recv, rs_send, rs_recv, w_sem, phase_sem):
    chips = n // 2
    far = chips // 2
    steps = 2 * far - 1
    layers = g1_ref.shape[0]
    rows, dim = tokens_ref.shape
    half_rows = rows // 2
    chip_rows = 2 * rows
    head = wout.shape[0]
    units = wup.shape[1]
    tile = min(512, dim)
    utile = min(512, units)

    me = lax.axis_index("tp")
    core = lax.rem(me, 2)
    chip = me // 2
    right, left = lax.rem(me + 2, n), lax.rem(me + n - 2, n)
    sibling = me + 1 - 2 * core
    target = (right, left)

    def slot_of(offset):
        if offset == 0:
            return 0
        if abs(offset) == far:
            return 1
        return 2 * abs(offset) + (1 if offset > 0 else 0)

    def signed(direction, distance):
        return -distance if direction == RIGHT else distance

    def ag_place(direction, m):
        distance = m // 2
        which = (m % 2) ^ direction
        return slot_of(signed(direction, distance)), slot_of(signed(direction, distance + 1)), pl.ds(which * half_rows, half_rows)

    def ag_copy(direction, m, width):
        src, dst, rws = ag_place(direction, m)
        return pltpu.make_async_remote_copy(
            src_ref=hbuf.at[src, core, rws, pl.ds(0, width)], dst_ref=hbuf.at[dst, core, rws, pl.ds(0, width)],
            send_sem=ag_send.at[direction, m], recv_sem=ag_recv.at[direction, m],
            device_id={"tp": target[direction]}, device_id_type=MESH)

    def sib_copy(direction, m, width):
        dst, rws = ag_place(direction, m)[1:]
        ref = hbuf.at[dst, core, rws, pl.ds(0, width)]
        return pltpu.make_async_remote_copy(
            src_ref=ref, dst_ref=ref, send_sem=sib_send.at[direction, m], recv_sem=sib_recv.at[direction, m],
            device_id={"tp": sibling}, device_id_type=MESH)

    def own_copy(width):
        ref = hbuf.at[0, core, pl.ds(0, rows), pl.ds(0, width)]
        return pltpu.make_async_remote_copy(
            src_ref=ref, dst_ref=ref, send_sem=own_sem.at[0], recv_sem=own_sem.at[1],
            device_id={"tp": sibling}, device_id_type=MESH)

    def part_copy(pair):
        return pltpu.make_async_remote_copy(
            src_ref=part.at[pl.ds(2 * pair, 2), 1 - core], dst_ref=psib.at[pl.ds(2 * pair, 2)],
            send_sem=part_send.at[pair], recv_sem=part_recv.at[pair],
            device_id={"tp": sibling}, device_id_type=MESH)

    def rs_plan(direction, m):
        if m == steps - 1:
            which, distance, before = 0, 1, m - 1
        elif m % 2 == 0:
            which, distance, before = 1, far - 1 - m // 2, m - 2
        else:
            which, distance, before = 0, far - m // 2, m - 2
        dest = slot_of(-signed(direction, distance))
        return which ^ direction, dest, (before if m >= 2 else None)

    def rs_copy(direction, m):
        before = rs_plan(direction, m)[2]
        src = fresh.at[direction, m] if before is None else ring.at[direction, before]
        return pltpu.make_async_remote_copy(
            src_ref=src, dst_ref=ring.at[direction, m], send_sem=rs_send.at[direction, m], recv_sem=rs_recv.at[direction, m],
            device_id={"tp": target[direction]}, device_id_type=MESH)

    def rs_step(m):
        for direction in (RIGHT, LEFT):
            which, dest, before = rs_plan(direction, m)
            if before is not None:
                rs_copy(direction, before).wait_recv()
            rws = pl.ds(which * half_rows, half_rows)

            def add(i):
                cs = cols_at(i, tile)
                total = part[dest, core, rws, cs].astype(F32) + psib[dest, rws, cs].astype(F32)
                if before is None:
                    fresh[direction, m, :, cs] = total
                else:
                    ring[direction, before, :, cs] = ring[direction, before, :, cs] + total

            loop(dim // tile, add)
            rs_copy(direction, m).start()

    def weight_copy(src, dst, index):
        return pltpu.make_async_copy(src, dst, w_sem.at[index])

    def signal_phase(sem):
        for device in (left, right, sibling):
            pl.semaphore_signal(sem, inc=1, device_id={"tp": device}, device_id_type=MESH)

    def norm(layer, gain_ref, shift_ref):
        for which in range(2):
            rws = pl.ds(which * half_rows, half_rows)

            def sum_body(i, acc):
                return acc + resid[rws, cols_at(i, tile)]

            total = lax.fori_loop(0, dim // tile, sum_body, jnp.zeros((half_rows, tile), F32))
            mean = jnp.sum(total, axis=1, keepdims=True) / dim

            def sq_body(i, acc):
                centered = resid[rws, cols_at(i, tile)] - mean
                return acc + centered * centered

            total = lax.fori_loop(0, dim // tile, sq_body, jnp.zeros((half_rows, tile), F32))
            scale = lax.rsqrt(jnp.sum(total, axis=1, keepdims=True) / dim + 1e-5)

            def out_body(i):
                cs = cols_at(i, tile)
                value = (resid[rws, cs] - mean) * scale * gain_ref[pl.ds(layer, 1), cs] + shift_ref[pl.ds(layer, 1), cs]
                hbuf[0, core, rws, cs] = value.astype(BF16)

            loop(dim // tile, out_body)

    def finish(layer, bias_ref):
        for which in range(2):
            last, early = (which, steps - 1), (1 - which, steps - 3)
            rs_copy(*early).wait_recv()
            rs_copy(*last).wait_recv()
            rws = pl.ds(which * half_rows, half_rows)

            def body(i):
                cs = cols_at(i, tile)
                total = part[0, core, rws, cs].astype(F32) + psib[0, rws, cs].astype(F32)
                total = total + ring[early[0], early[1], :, cs] + ring[last[0], last[1], :, cs]
                resid[rws, cs] = resid[rws, cs] + (total + bias_ref[pl.ds(layer, 1), cs])

            loop(dim // tile, body)
        for m in range(steps):
            for direction in (RIGHT, LEFT):
                rs_copy(direction, m).wait_send()
        for pair in range(far):
            part_copy(pair).wait_send()
        signal_phase(phase_sem)

    def pair_rows(pair):
        return hbuf[pl.ds(2 * pair, 2), :, :, pl.ds(0, dim)].reshape(2 * chip_rows, dim)

    def gather_start(width):
        for m in (0, 1):
            for direction in (RIGHT, LEFT):
                ag_copy(direction, m, width).start()
        own_copy(width).start()

    def gather_step(m, width):
        for direction in (RIGHT, LEFT):
            ag_copy(direction, m, width).wait_recv()
            if m + 2 < steps:
                ag_copy(direction, m + 2, width).start()
            sib_copy(direction, m, width).start()

    def sib_wait(m, width):
        for direction in (RIGHT, LEFT):
            sib_copy(direction, m, width).wait_recv()

    def gather_end(width):
        own_copy(width).wait_send()
        for m in range(steps):
            for direction in (RIGHT, LEFT):
                ag_copy(direction, m, width).wait_send()
                sib_copy(direction, m, width).wait_send()

    def exchange(width, first_half, second_half, prepare, finish_pair):
        gather_start(width)
        for m in range(steps):
            gather_step(m, width)
            if m % 2 == 1:
                sib_wait(m - 1, width)
                sib_wait(m, width)
                first_half(m // 2 + 1)
                if m == steps - 2:
                    second_half(far - 1)
            elif m >= 2 and m < steps - 1:
                second_half(m // 2)
        own_copy(width).wait_recv()
        prepare(steps - 1, width)
        finish_pair(far - 1)
        part_copy(far - 1).start()
        part_copy(far - 1).wait_recv()
        rs_step(0)

    def attention_half(layer):
        width = dim + ID_COLS

        def project(pair):
            lhs = pair_rows(pair)

            def body(t):
                value = jnp.dot(lhs, wqkv[t], preferred_element_type=F32).astype(BF16)
                qkv[t, pl.ds(2 * pair, 2)] = value.reshape(2, chip_rows, head)

            loop(3, body)

        def attend(pair):
            def body(i):
                slot = 2 * pair + i
                keys = qkv[1].reshape(chips * chip_rows, head)
                values = qkv[2].reshape(chips * chip_rows, head)
                scores = lax.dot_general(qkv[0, slot], keys, (((1,), (1,)), ((), ())), preferred_element_type=F32) * (head ** -0.5)
                ids_col = hbuf[slot, :, :, pl.ds(dim, ID_COLS)].astype(F32).reshape(chip_rows, ID_COLS)[:, 0:1]
                base = slot_chip(pair, i) * chip_rows
                pos_col = lax.broadcasted_iota(jnp.int32, (chip_rows, 1), 0) + base
                allowed = (kpos[0:1, :] <= pos_col) & (kids[0:1, :] == ids_col)
                scores = jnp.where(allowed, scores, -1e30)
                top = jnp.max(scores, axis=1, keepdims=True)
                probs = jnp.exp(scores - top)
                probs = (probs * (1.0 / jnp.sum(probs, axis=1, keepdims=True))).astype(BF16)
                mixed = jnp.dot(probs, values, preferred_element_type=F32).astype(BF16)

                def proj(c):
                    cs = cols_at(c, tile)
                    value = jnp.dot(mixed, wout[:, cs], preferred_element_type=F32).astype(BF16)
                    part[slot, :, :, cs] = value.reshape(2, rows, tile)

                loop(dim // tile, proj)

            loop(2, body)

        def slot_chip(pair, i):
            if pair == 0:
                return lax.rem(chip + i * far, chips)
            return lax.rem(chip + chips + (2 * i - 1) * pair, chips)

        def prepare(m, width):
            sib_wait(m, width)
            project(0)
            for pair in range(far):
                for i in range(2):
                    slot = 2 * pair + i
                    cs = pl.ds(slot * chip_rows, chip_rows)
                    kpos[:, cs] = lax.broadcasted_iota(jnp.int32, (8, chip_rows), 1) + slot_chip(pair, i) * chip_rows
                    block = hbuf[slot, :, :, pl.ds(dim, ID_COLS)].astype(F32).reshape(chip_rows, ID_COLS)
                    kids[:, cs] = block.T[0:8, :]

        weight_copy(wup_hbm.at[layer], wup, 2).start()
        weight_copy(wdown_hbm.at[layer], wdown, 3).start()
        weight_copy(wqkv_hbm.at[layer], wqkv, 0).wait()
        weight_copy(wout_hbm.at[layer], wout, 1).wait()
        exchange(width, project, lambda pair: None, prepare, attend)
        attend(0)
        part_copy(0).start()
        part_copy(0).wait_recv()
        rs_step(1)
        for pair in range(far - 2, 0, -1):
            attend(pair)
            part_copy(pair).start()
            part_copy(pair).wait_recv()
            first = 2 * (far - 1 - pair)
            rs_step(first)
            rs_step(first + 1)
        rs_step(steps - 1)
        gather_end(width)

    def mlp_half(layer):
        width = dim

        def up(pair):
            lhs = pair_rows(pair)

            def body(c):
                cs = cols_at(c, utile)
                x = jnp.dot(lhs, wup[:, cs], preferred_element_type=F32) + ub_ref[pl.ds(layer, 1), cs]
                inner = 0.7978845608028654 * (x + 0.044715 * (x * x * x))
                hidden[:, cs] = (0.5 * x * (1.0 + jnp.tanh(inner))).astype(BF16)

            loop(units // utile, body)

        def down(pair):
            def body(c):
                cs = cols_at(c, tile)
                value = jnp.dot(hidden[...], wdown[:, cs], preferred_element_type=F32).astype(BF16)
                part[pl.ds(2 * pair, 2), :, :, cs] = value.reshape(2, 2, rows, tile)

            loop(dim // tile, body)
            if pair != far - 1:
                part_copy(pair).start()

        weight_copy(wup_hbm.at[layer], wup, 2).wait()
        weight_copy(wdown_hbm.at[layer], wdown, 3).wait()

        @pl.when(layer + 1 < layers)
        def _():
            weight_copy(wqkv_hbm.at[layer + 1], wqkv, 0).start()
            weight_copy(wout_hbm.at[layer + 1], wout, 1).start()

        exchange(width, up, down, lambda m, width: None, lambda pair: None)
        sib_wait(steps - 1, width)
        up(0)
        down(0)
        part_copy(0).wait_recv()
        rs_step(1)
        for pair in range(far - 2, 0, -1):
            part_copy(pair).wait_recv()
            first = 2 * (far - 1 - pair)
            rs_step(first)
            rs_step(first + 1)
        rs_step(steps - 1)
        gather_end(width)

    weight_copy(wqkv_hbm.at[0], wqkv, 0).start()
    weight_copy(wout_hbm.at[0], wout, 1).start()
    barrier = pltpu.get_barrier_semaphore()
    signal_phase(barrier)
    for which in range(2):
        rws = pl.ds(which * half_rows, half_rows)
        loop(dim // tile, lambda i: resid.__setitem__((rws, cols_at(i, tile)), tokens_ref[rws, cols_at(i, tile)].astype(F32)))
    hbuf[0, core, :, pl.ds(dim, ID_COLS)] = ids_ref[...]
    norm(0, g1_ref, s1_ref)
    pl.semaphore_wait(barrier, 3)

    def layer_body(layer):
        attention_half(layer)
        finish(layer, ob_ref)
        norm(layer, g2_ref, s2_ref)
        pl.semaphore_wait(phase_sem, 3)
        mlp_half(layer)
        finish(layer, db_ref)
        norm(lax.rem(layer + 1, layers), g1_ref, s1_ref)
        pl.semaphore_wait(phase_sem, 3)

    loop(layers, layer_body)
    loop(dim // tile, lambda i: out_ref.__setitem__((slice(None), cols_at(i, tile)), resid[:, cols_at(i, tile)].astype(BF16)))


def solution(mesh):
    n = mesh.shape["tp"]
    chips = n // 2
    far = chips // 2
    steps = 2 * far - 1
    row_spec = P("dp", "tp", None)
    vec_spec = P(None, None)
    in_specs = (row_spec, P("dp", "tp"), vec_spec, vec_spec, P(None, None, None, "tp", None), P(None, "tp", None, None), vec_spec, vec_spec, vec_spec, P(None, None, "tp"), P(None, "tp"), P(None, "tp", None), vec_spec)

    def device_fn(tokens, doc_ids, norm1_gain, norm1_shift, qkv_weight, out_weight, out_bias, norm2_gain, norm2_shift, up_weight, up_bias, down_weight, down_bias):
        batch, rows, dim = tokens.shape
        layers = norm1_gain.shape[0]
        head = qkv_weight.shape[-1]
        units = up_weight.shape[-1]
        ids = jnp.broadcast_to(doc_ids.reshape(rows, 1).astype(BF16), (rows, ID_COLS))
        wqkv = jnp.transpose(qkv_weight, (0, 2, 3, 1, 4)).reshape(layers, 3, dim, head)
        wout = out_weight.reshape(layers, head, dim)
        vmem = pl.BlockSpec(memory_space=pltpu.VMEM)
        hbm = pl.BlockSpec(memory_space=pl.ANY)
        dma = pltpu.SemaphoreType.DMA
        result = pl.pallas_call(
            functools.partial(block_kernel, n),
            out_shape=jax.ShapeDtypeStruct((rows, dim), BF16),
            in_specs=[vmem] * 9 + [hbm] * 4,
            out_specs=vmem,
            scratch_shapes=[
                pltpu.VMEM((chips, 2, rows, dim + ID_COLS), BF16),
                pltpu.VMEM((chips, 2, rows, dim), BF16),
                pltpu.VMEM((chips, rows, dim), BF16),
                pltpu.VMEM((2, steps, rows // 2, dim), F32),
                pltpu.VMEM((2, 2, rows // 2, dim), F32),
                pltpu.VMEM((rows, dim), F32),
                pltpu.VMEM((3, dim, head), BF16),
                pltpu.VMEM((head, dim), BF16),
                pltpu.VMEM((dim, units), BF16),
                pltpu.VMEM((units, dim), BF16),
                pltpu.VMEM((3, chips, 2 * rows, head), BF16),
                pltpu.VMEM((4 * rows, units), BF16),
                pltpu.VMEM((8, chips * 2 * rows), jnp.int32),
                pltpu.VMEM((8, chips * 2 * rows), F32),
                dma((2, steps)), dma((2, steps)), dma((2, steps)), dma((2, steps)), dma((2,)),
                dma((far,)), dma((far,)), dma((2, steps)), dma((2, steps)), dma((4,)),
                pltpu.SemaphoreType.REGULAR,
            ],
            compiler_params=pltpu.CompilerParams(collective_id=0, has_side_effects=True, vmem_limit_bytes=67043328),
        )(tokens.reshape(rows, dim), ids, norm1_gain, norm1_shift, out_bias, norm2_gain, norm2_shift, up_bias, down_bias, wqkv, wout, up_weight, down_weight)
        return result.reshape(batch, rows, dim)

    return jax.shard_map(device_fn, mesh=mesh, in_specs=in_specs, out_specs=row_spec, check_vma=False)
```

time: 734 us -> 554 us (0.75)
  waiting for transfers between devices: 574 us -> 0 us
  Pallas kernels: 0 us -> 549 us
  matrix products: 101 us -> 0 us
  other arithmetic: 19.5 us -> 0.66 us
  blocking collectives: 16.1 us -> 0 us
  between operations: 14.4 us -> 0.01 us
    pallas_call x0 -> x1, Pallas kernels: none -> 549 us  [device_fn(): pl.pallas_call(functools.partial(block_kernel, n), out_shape=jax.ShapeDty...]
    reduce_scatter x4 -> x0, waiting for transfers between devices: 378 us -> none  [scatter_sum(): lax.psum_scatter(partial_rows.astype(jnp.float32), 'tp', scatter_dimensio...]
    all_gather x4 -> x0, waiting for transfers between devices: 195 us -> none  [the longest x2 104 us: device_fn(): full_rows2 = lax.all_gather(normed2, 'tp', axis=1, tiled=True)]
    dot_general x16 -> x0, matrix products: 101 us -> none  [the longest x2 29.2 us: device_fn(): jnp.einsum('bsd,df->bsf', full_rows2, up_weight[layer_idx], preferred_ele...]
    unnamed x1 -> x0, blocking collectives: 16.1 us -> none
    reduce_sum x12 -> x0, other arithmetic: 10.7 us -> none  [the longest x4 5.84 us: layer_norm(): mean_val = jnp.mean(residual, axis=-1, keepdims=True)]
    convert_element_type x5 -> x1, other arithmetic: 8.69 us -> 0.66 us  [device_fn(): doc_ids.reshape(rows, 1).astype(BF16)]
  transfers between devices with their start and end apart: 8 -> 0, of which waited for: 8 -> 0; matrix products, arithmetic and copies ran while one was open for 0% -> 0% of each run, Pallas kernels for 0% -> 0%
where the time goes in v2:
time: 554 us; the launch traced here: 552 us
  Pallas kernels  549 us (99%)
    pallas_call x1, Pallas kernels, device_fn(): pl.pallas_call(functools.partial(block_kernel, n), out_shape=jax.ShapeDty...  549 us

profile of v2, /device:TPU:21, one launch (start us, length us, event | category | flops | bytes accessed | tf_op | source)
XLA Modules:
  0.0 552.3 jit_solution(8677205707252340163)
XLA Ops:
  0.0 0.7 convert_bitcast_fusion
  0.7 0.7 broadcast_in_dim.2.ids_ref
  1.3 549.1 %shard_map.127 = bf16[64,4096]{1,0:T(8,128)(2,1)} custom-call(bf16[64,4096]{1,0:T(8,128)(2,1)} %bitcast.13, bf16[64,128]{1,0:T(8,128)(2,1)} %broadcast_in_dim.2.ids_ref, f32[2,4096]{1,0:T(2,128)} %g1_ref.1, f32[2,4096]{1,0:T(2,128)} %s1_ref.1, f32[2,4096]{1,0:T(2,128)} %ob_ref.1, f32[2,4096]{1,0:T(2,128)} %g2_ref.1, f32[2,4096]{1,0:T(2,128)} %s2_ref.1, ...), custom_call_target="tpu_custom_call" | custom-call | tf_op jit(solution)/shard_map/pallas_call | solution.py:383
  550.4 1.9 copy.16

commit v3 on v1

v3 whole, which is shorter than its diff:
```python
import functools

import jax
import jax.numpy as jnp
from jax import lax
from jax.experimental import pallas as pl
from jax.experimental.pallas import tpu as pltpu
from jax.sharding import PartitionSpec as P

MESH = pl.DeviceIdType.MESH
F32, BF16 = jnp.float32, jnp.bfloat16
ID_COLS = 128
RIGHT, LEFT = 0, 1


def loop(count, body):
    lax.fori_loop(0, count, lambda i, carry: (body(i), carry)[1], 0)


def cols_at(i, width):
    return pl.ds(pl.multiple_of(i * width, width), width)


def block_kernel(n, tokens_ref, ids_ref, g1_ref, s1_ref, ob_ref, g2_ref, s2_ref, ub_ref, db_ref, wqkv_hbm, wout_hbm, wup_hbm, wdown_hbm,
                 out_ref, hbuf, part, psib, ring, fresh, resid, wqkv, wout, wup, wdown, qkv, hidden, kpos, kids,
                 ag_send, ag_recv, sib_send, sib_recv, own_send, own_recv, part_send, part_recv, rs_send, rs_recv, w_sem):
    chips = n // 2
    far = chips // 2
    steps = 2 * far - 1
    layers = g1_ref.shape[0]
    rows, dim = tokens_ref.shape
    half_rows, quarter = rows // 2, rows // 4
    chip_rows = 2 * rows
    head = wout.shape[0]
    units = wup.shape[1]
    tile = min(512, dim)
    utile = min(512, units)

    me = lax.axis_index("tp")
    core = lax.rem(me, 2)
    chip = me // 2
    right, left = lax.rem(me + 2, n), lax.rem(me + n - 2, n)
    sibling = me + 1 - 2 * core
    target = (right, left)

    def slot_of(offset):
        if offset == 0:
            return 0
        if abs(offset) == far:
            return 1
        return 2 * abs(offset) + (1 if offset > 0 else 0)

    def slot_chip(slot):
        if slot == 0:
            return chip
        if slot == 1:
            return lax.rem(chip + far, chips)
        offset = slot // 2 if slot % 2 else -(slot // 2)
        return lax.rem(chip + chips + offset, chips)

    def signed(direction, distance):
        return -distance if direction == RIGHT else distance

    def quarter_rows(which, t):
        return pl.ds(which * half_rows + t * quarter, quarter)

    def half_ds(which):
        return pl.ds(which * half_rows, half_rows)

    def messages(direction):
        a, b = direction, 1 - direction
        out = [(0, a, 0), (0, b, 0), (0, a, 1), (0, b, 1)]
        for j in range(1, far - 1):
            out += [(j, a, 0), (j, a, 1), (j, b, 0), (j, b, 1)]
        return out + [(far - 1, a, 0), (far - 1, a, 1)]

    plans = (messages(RIGHT), messages(LEFT))
    count = len(plans[0])

    def width_of(which, t, with_ids):
        return dim + ID_COLS if with_ids and which == 0 and t == 0 else dim

    def ag_ref(direction, m, extra, with_ids):
        j, which, t = plans[direction][m]
        return hbuf.at[slot_of(signed(direction, j + extra)), core, quarter_rows(which, t), pl.ds(0, width_of(which, t, with_ids))]

    def ag_copy(direction, m, with_ids):
        return pltpu.make_async_remote_copy(
            src_ref=ag_ref(direction, m, 0, with_ids), dst_ref=ag_ref(direction, m, 1, with_ids),
            send_sem=ag_send.at[direction, m], recv_sem=ag_recv.at[direction, m],
            device_id={"tp": target[direction]}, device_id_type=MESH)

    def sib_copy(direction, m, with_ids):
        ref = ag_ref(direction, m, 1, with_ids)
        return pltpu.make_async_remote_copy(
            src_ref=ref, dst_ref=ref, send_sem=sib_send.at[direction, m], recv_sem=sib_recv.at[direction, m],
            device_id={"tp": sibling}, device_id_type=MESH)

    def own_copy(which, t, with_ids):
        ref = hbuf.at[0, core, quarter_rows(which, t), pl.ds(0, width_of(which, t, with_ids))]
        return pltpu.make_async_remote_copy(
            src_ref=ref, dst_ref=ref, send_sem=own_send.at[which, t], recv_sem=own_recv.at[which, t],
            device_id={"tp": sibling}, device_id_type=MESH)

    def part_copy(piece):
        slot, which = piece
        return pltpu.make_async_remote_copy(
            src_ref=part.at[slot, 1 - core, half_ds(which)], dst_ref=psib.at[slot, half_ds(which)],
            send_sem=part_send.at[slot, which], recv_sem=part_recv.at[slot, which],
            device_id={"tp": sibling}, device_id_type=MESH)

    def rs_plan(direction, m):
        if m == steps - 1:
            which, distance, before = 0, 1, m - 1
        elif m % 2 == 0:
            which, distance, before = 1, far - 1 - m // 2, m - 2
        else:
            which, distance, before = 0, far - m // 2, m - 2
        dest = slot_of(-signed(direction, distance))
        return which ^ direction, dest, (before if m >= 2 else None)

    def rs_copy(direction, m, t):
        before = rs_plan(direction, m)[2]
        src = fresh.at[direction, m, t] if before is None else ring.at[direction, before, t]
        return pltpu.make_async_remote_copy(
            src_ref=src, dst_ref=ring.at[direction, m, t], send_sem=rs_send.at[direction, m, t], recv_sem=rs_recv.at[direction, m, t],
            device_id={"tp": target[direction]}, device_id_type=MESH)

    def rs_step(m, need):
        for direction in (RIGHT, LEFT):
            which, dest, before = rs_plan(direction, m)
            need((dest, which))
        for t in range(2):
            for direction in (RIGHT, LEFT):
                which, dest, before = rs_plan(direction, m)
                if before is not None:
                    rs_copy(direction, before, t).wait_recv()
                rws = quarter_rows(which, t)

                def add(i):
                    cs = cols_at(i, tile)
                    total = part[dest, core, rws, cs].astype(F32) + psib[dest, rws, cs].astype(F32)
                    if before is None:
                        fresh[direction, m, t, :, cs] = total
                    else:
                        ring[direction, before, t, :, cs] = ring[direction, before, t, :, cs] + total

                loop(dim // tile, add)
                rs_copy(direction, m, t).start()

    def weight_copy(src, dst, index):
        return pltpu.make_async_copy(src, dst, w_sem.at[index])

    def norm_send(t, sums, layer, gain_ref, shift_ref, with_ids, before_send=None):
        means = [jnp.sum(s, axis=1, keepdims=True) / dim for s in sums]

        def sq_body(i, acc):
            out = []
            for which in range(2):
                centered = resid[quarter_rows(which, t), cols_at(i, tile)] - means[which]
                out.append(acc[which] + centered * centered)
            return tuple(out)

        zero = jnp.zeros((quarter, tile), F32)
        squares = lax.fori_loop(0, dim // tile, sq_body, (zero, zero))
        scales = [lax.rsqrt(jnp.sum(s, axis=1, keepdims=True) / dim + 1e-5) for s in squares]

        def out_body(i):
            cs = cols_at(i, tile)
            for which in range(2):
                rws = quarter_rows(which, t)
                value = (resid[rws, cs] - means[which]) * scales[which] * gain_ref[pl.ds(layer, 1), cs] + shift_ref[pl.ds(layer, 1), cs]
                hbuf[0, core, rws, cs] = value.astype(BF16)

        loop(dim // tile, out_body)
        if before_send is not None:
            before_send()
        for i in range(2):
            for direction in (RIGHT, LEFT):
                ag_copy(direction, 2 * t + i, with_ids).start()
        for which in range(2):
            own_copy(which, t, with_ids).start()

    def finish(t, layer, bias_ref):
        for which in range(2):
            rs_copy(1 - which, steps - 3, t).wait_recv()
            rs_copy(which, steps - 1, t).wait_recv()

        def body(i, acc):
            cs = cols_at(i, tile)
            out = []
            for which in range(2):
                rws = quarter_rows(which, t)
                total = part[0, core, rws, cs].astype(F32) + psib[0, rws, cs].astype(F32)
                total = total + ring[1 - which, steps - 3, t, :, cs] + ring[which, steps - 1, t, :, cs]
                value = resid[rws, cs] + (total + bias_ref[pl.ds(layer, 1), cs])
                resid[rws, cs] = value
                out.append(acc[which] + value)
            return tuple(out)

        zero = jnp.zeros((quarter, tile), F32)
        return lax.fori_loop(0, dim // tile, body, (zero, zero))

    def boundary(layer, bias_ref, next_layer, gain_ref, shift_ref, with_ids, more=None):
        for t in range(2):
            sums = finish(t, layer, bias_ref)
            if more is None:
                norm_send(t, sums, next_layer, gain_ref, shift_ref, with_ids)
            else:
                @pl.when(more)
                def _():
                    norm_send(t, sums, next_layer, gain_ref, shift_ref, with_ids)
        for m in range(steps):
            for direction in (RIGHT, LEFT):
                for t in range(2):
                    rs_copy(direction, m, t).wait_send()
        for slot in range(chips):
            for which in range(2):
                part_copy((slot, which)).wait_send()

    def needs():
        seen = set()

        def need(piece):
            if piece not in seen:
                seen.add(piece)
                part_copy(piece).wait_recv()

        return need

    def gather_step(m, with_ids):
        for direction in (RIGHT, LEFT):
            ag_copy(direction, m, with_ids).wait_recv()
            j, which, t = plans[direction][m]
            if (j + 1, which, t) in plans[direction]:
                ag_copy(direction, plans[direction].index((j + 1, which, t)), with_ids).start()
            sib_copy(direction, m, with_ids).start()

    def sib_wait(first, last, with_ids):
        for m in range(first, last + 1):
            for direction in (RIGHT, LEFT):
                sib_copy(direction, m, with_ids).wait_recv()

    def own_wait(with_ids):
        for which in range(2):
            for t in range(2):
                own_copy(which, t, with_ids).wait_recv()

    def gather_end(with_ids):
        for which in range(2):
            for t in range(2):
                own_copy(which, t, with_ids).wait_send()
        for m in range(count):
            for direction in (RIGHT, LEFT):
                ag_copy(direction, m, with_ids).wait_send()
                sib_copy(direction, m, with_ids).wait_send()

    def load_rows(pieces):
        return jnp.concatenate([hbuf[s, :, half_ds(w), pl.ds(0, dim)].reshape(rows, dim) for s, w in pieces], axis=0)

    def store_part(pieces, value, cs):
        for i, (s, w) in enumerate(pieces):
            part[s, :, half_ds(w), cs] = value[i * rows:(i + 1) * rows].reshape(2, half_rows, tile)

    def both(slot):
        return [(slot, 0), (slot, 1)]

    minus, plus = slot_of(-(far - 1)), slot_of(far - 1)
    own = both(0)
    farthest = both(1)
    leading = [(minus, 0), (plus, 1)]
    trailing = [(minus, 1), (plus, 0)]

    def near(p):
        return both(2 * p) + both(2 * p + 1)

    lead_at = 4 * (far - 2) + 1
    last_at = count - 1

    def send_parts(pieces):
        for piece in pieces:
            part_copy(piece).start()

    def attention_half(layer):
        need = needs()

        def project(pieces, kinds=(0, 3)):
            def body(t):
                value = jnp.dot(load_rows(pieces), wqkv[t], preferred_element_type=F32).astype(BF16)
                for i, (s, w) in enumerate(pieces):
                    qkv[t, s, :, half_ds(w)] = value[i * rows:(i + 1) * rows].reshape(2, half_rows, head)

            lax.fori_loop(kinds[0], kinds[1], lambda t, carry: (body(t), carry)[1], 0)

        def slot_ids(slot):
            cs = pl.ds(slot * chip_rows, chip_rows)
            lines = [hbuf[slot, c, pl.ds(0, 8), pl.ds(dim, ID_COLS)].astype(F32)[:, 0:rows] for c in range(2)]
            kids[:, cs] = jnp.concatenate(lines, axis=1)

        def column_ids(piece):
            slot, which = piece
            line = kids[0:1, pl.ds(slot * chip_rows, chip_rows)]
            column = jnp.broadcast_to(line, (chip_rows, chip_rows)).T[:, 0:1]
            return jnp.concatenate([column[c * rows + which * half_rows:c * rows + (which + 1) * half_rows] for c in range(2)], axis=0)

        def column_pos(piece):
            slot, which = piece
            i = lax.broadcasted_iota(jnp.int32, (rows, 1), 0)
            i = i + jnp.where(i >= half_rows, rows - half_rows, 0)
            return i + (which * half_rows + slot_chip(slot) * chip_rows)

        def attend(pieces):
            keys = qkv[1].reshape(chips * chip_rows, head)
            values = qkv[2].reshape(chips * chip_rows, head)
            queries = jnp.concatenate([qkv[0, s, :, half_ds(w)].reshape(rows, head) for s, w in pieces], axis=0)
            scores = lax.dot_general(queries, keys, (((1,), (1,)), ((), ())), preferred_element_type=F32) * (head ** -0.5)
            ids_col = jnp.concatenate([column_ids(piece) for piece in pieces], axis=0)
            pos_col = jnp.concatenate([column_pos(piece) for piece in pieces], axis=0)
            allowed = (kpos[0:1, :] <= pos_col) & (kids[0:1, :] == ids_col)
            scores = jnp.where(allowed, scores, -1e30)
            top = jnp.max(scores, axis=1, keepdims=True)
            probs = jnp.exp(scores - top)
            probs = (probs * (1.0 / jnp.sum(probs, axis=1, keepdims=True))).astype(BF16)
            mixed = jnp.dot(probs, values, preferred_element_type=F32).astype(BF16)

            def proj(c):
                cs = cols_at(c, tile)
                store_part(pieces, jnp.dot(mixed, wout[:, cs], preferred_element_type=F32).astype(BF16), cs)

            loop(dim // tile, proj)

        weight_copy(wup_hbm.at[layer], wup, 2).start()
        weight_copy(wdown_hbm.at[layer], wdown, 3).start()
        weight_copy(wqkv_hbm.at[layer], wqkv, 0).wait()
        weight_copy(wout_hbm.at[layer], wout, 1).wait()
        for m in range(count):
            gather_step(m, True)
            if m == 0:
                own_wait(True)
                project(own)
                slot_ids(0)
            for p in range(1, far - 1):
                if m == 4 * p:
                    sib_wait(4 * p - 4, 4 * p - 1, True)
                    project(near(p))
                    slot_ids(2 * p)
                    slot_ids(2 * p + 1)
            if m == last_at - 2:
                sib_wait(lead_at - 1, m, True)
                project(leading + trailing)
                slot_ids(minus)
                slot_ids(plus)
        sib_wait(last_at - 1, last_at, True)
        project(farthest, (1, 3))
        slot_ids(1)
        attend(leading)
        send_parts(leading)
        project(farthest, (0, 1))
        rs_step(0, need)
        attend(farthest)
        send_parts(farthest)
        rs_step(1, need)
        for pieces in [trailing] + [both(2 * p + i) for p in range(far - 2, 0, -1) for i in range(2)]:
            attend(pieces)
            send_parts(pieces)
        gather_end(True)
        attend(own)
        send_parts(own)
        for m in range(2, steps):
            rs_step(m, need)
        for piece in own:
            need(piece)

    def mlp_half(layer):
        need = needs()

        def up(pieces):
            count_rows = rows * len(pieces)

            def body(c):
                cs = cols_at(c, utile)
                x = jnp.dot(load_rows(pieces), wup[:, cs], preferred_element_type=F32) + ub_ref[pl.ds(layer, 1), cs]
                inner = 0.7978845608028654 * (x + 0.044715 * (x * x * x))
                hidden[pl.ds(0, count_rows), cs] = (0.5 * x * (1.0 + jnp.tanh(inner))).astype(BF16)

            loop(units // utile, body)

        def down(pieces):
            count_rows = rows * len(pieces)

            def body(c):
                cs = cols_at(c, tile)
                value = jnp.dot(hidden[pl.ds(0, count_rows), :], wdown[:, cs], preferred_element_type=F32).astype(BF16)
                store_part(pieces, value, cs)

            loop(dim // tile, body)

        weight_copy(wup_hbm.at[layer], wup, 2).wait()
        weight_copy(wdown_hbm.at[layer], wdown, 3).wait()

        @pl.when(layer + 1 < layers)
        def _():
            weight_copy(wqkv_hbm.at[layer + 1], wqkv, 0).start()
            weight_copy(wout_hbm.at[layer + 1], wout, 1).start()

        for m in range(last_at):
            gather_step(m, False)
            if m == 0:
                own_wait(False)
                up(own)
            if m == 1:
                down(own)
                send_parts(own)
            for p in range(1, far - 1):
                if m == 4 * p:
                    sib_wait(4 * p - 4, 4 * p - 1, False)
                    up(near(p))
                if m == 4 * p + (0 if p == far - 2 else 1):
                    down(near(p))
                    send_parts(near(p))
            if m == lead_at:
                sib_wait(lead_at - 1, lead_at, False)
                up(leading)
                down(leading)
                send_parts(leading)
        rs_step(0, need)
        gather_step(last_at, False)
        sib_wait(lead_at + 1, last_at, False)
        up(farthest + trailing)
        down(farthest + trailing)
        gather_end(False)
        send_parts(farthest + trailing)
        for m in range(1, steps):
            rs_step(m, need)
        for slot in range(chips):
            for piece in both(slot):
                need(piece)

    weight_copy(wqkv_hbm.at[0], wqkv, 0).start()
    weight_copy(wout_hbm.at[0], wout, 1).start()
    barrier = pltpu.get_barrier_semaphore()
    for device in (left, right, sibling):
        pl.semaphore_signal(barrier, inc=1, device_id={"tp": device}, device_id_type=MESH)
    hbuf[0, core, pl.ds(0, quarter), pl.ds(dim, ID_COLS)] = jnp.zeros((quarter, ID_COLS), BF16)
    hbuf[0, core, pl.ds(0, quarter), pl.ds(dim, rows)] = jnp.broadcast_to(ids_ref[...].astype(F32).astype(BF16), (quarter, rows))
    for slot in range(chips):
        kpos[:, pl.ds(slot * chip_rows, chip_rows)] = lax.broadcasted_iota(jnp.int32, (8, chip_rows), 1) + slot_chip(slot) * chip_rows
    for t in range(2):
        def widen(i, acc):
            out = []
            for which in range(2):
                rws = quarter_rows(which, t)
                value = tokens_ref[rws, cols_at(i, tile)].astype(F32)
                resid[rws, cols_at(i, tile)] = value
                out.append(acc[which] + value)
            return tuple(out)

        zero = jnp.zeros((quarter, tile), F32)
        sums = lax.fori_loop(0, dim // tile, widen, (zero, zero))
        norm_send(t, sums, 0, g1_ref, s1_ref, True, (lambda: pl.semaphore_wait(barrier, 3)) if t == 0 else None)

    def layer_body(layer):
        attention_half(layer)
        boundary(layer, ob_ref, layer, g2_ref, s2_ref, False)
        mlp_half(layer)
        boundary(layer, db_ref, lax.rem(layer + 1, layers), g1_ref, s1_ref, True, layer + 1 < layers)

    loop(layers, layer_body)
    loop(dim // tile, lambda i: out_ref.__setitem__((slice(None), cols_at(i, tile)), resid[:, cols_at(i, tile)].astype(BF16)))


def solution(mesh):
    n = mesh.shape["tp"]
    chips = n // 2
    far = chips // 2
    steps = 2 * far - 1
    sends = 4 * far - 2
    row_spec = P("dp", "tp", None)
    vec_spec = P(None, None)
    in_specs = (row_spec, P("dp", "tp"), vec_spec, vec_spec, P(None, None, None, "tp", None), P(None, "tp", None, None), vec_spec, vec_spec, vec_spec, P(None, None, "tp"), P(None, "tp"), P(None, "tp", None), vec_spec)

    def device_fn(tokens, doc_ids, norm1_gain, norm1_shift, qkv_weight, out_weight, out_bias, norm2_gain, norm2_shift, up_weight, up_bias, down_weight, down_bias):
        batch, rows, dim = tokens.shape
        layers = norm1_gain.shape[0]
        head = qkv_weight.shape[-1]
        units = up_weight.shape[-1]
        wqkv = jnp.transpose(qkv_weight, (0, 2, 3, 1, 4)).reshape(layers, 3, dim, head)
        wout = out_weight.reshape(layers, head, dim)
        vmem = pl.BlockSpec(memory_space=pltpu.VMEM)
        hbm = pl.BlockSpec(memory_space=pl.ANY)
        dma = pltpu.SemaphoreType.DMA
        result = pl.pallas_call(
            functools.partial(block_kernel, n),
            out_shape=jax.ShapeDtypeStruct((rows, dim), BF16),
            in_specs=[vmem] * 9 + [hbm] * 4,
            out_specs=vmem,
            scratch_shapes=[
                pltpu.VMEM((chips, 2, rows, dim + ID_COLS), BF16),
                pltpu.VMEM((chips, 2, rows, dim), BF16),
                pltpu.VMEM((chips, rows, dim), BF16),
                pltpu.VMEM((2, steps, 2, rows // 4, dim), F32),
                pltpu.VMEM((2, 2, 2, rows // 4, dim), F32),
                pltpu.VMEM((rows, dim), F32),
                pltpu.VMEM((3, dim, head), BF16),
                pltpu.VMEM((head, dim), BF16),
                pltpu.VMEM((dim, units), BF16),
                pltpu.VMEM((units, dim), BF16),
                pltpu.VMEM((3, chips, 2, rows, head), BF16),
                pltpu.VMEM((4 * rows, units), BF16),
                pltpu.VMEM((8, chips * 2 * rows), jnp.int32),
                pltpu.VMEM((8, chips * 2 * rows), F32),
                dma((2, sends)), dma((2, sends)), dma((2, sends)), dma((2, sends)), dma((2, 2)), dma((2, 2)),
                dma((chips, 2)), dma((chips, 2)), dma((2, steps, 2)), dma((2, steps, 2)), dma((4,)),
            ],
            compiler_params=pltpu.CompilerParams(collective_id=0, has_side_effects=True, vmem_limit_bytes=67043328),
        )(tokens.reshape(rows, dim), doc_ids, norm1_gain, norm1_shift, out_bias, norm2_gain, norm2_shift, up_bias, down_bias, wqkv, wout, up_weight, down_weight)
        return result.reshape(batch, rows, dim)

    return jax.shard_map(device_fn, mesh=mesh, in_specs=in_specs, out_specs=row_spec, check_vma=False)
```

time: 734 us -> 515 us (0.70)
  waiting for transfers between devices: 574 us -> 0 us
  Pallas kernels: 0 us -> 513 us
  matrix products: 101 us -> 0 us
  other arithmetic: 19.5 us -> 0 us
  blocking collectives: 16.1 us -> 0 us
  between operations: 14.4 us -> 0.01 us
    pallas_call x0 -> x1, Pallas kernels: none -> 513 us  [device_fn(): pl.pallas_call(functools.partial(block_kernel, n), out_shape=jax.ShapeDty...]
    reduce_scatter x4 -> x0, waiting for transfers between devices: 378 us -> none  [scatter_sum(): lax.psum_scatter(partial_rows.astype(jnp.float32), 'tp', scatter_dimensio...]
    all_gather x4 -> x0, waiting for transfers between devices: 195 us -> none  [the longest x2 104 us: device_fn(): full_rows2 = lax.all_gather(normed2, 'tp', axis=1, tiled=True)]
    dot_general x16 -> x0, matrix products: 101 us -> none  [the longest x2 29.2 us: device_fn(): jnp.einsum('bsd,df->bsf', full_rows2, up_weight[layer_idx], preferred_ele...]
    unnamed x1 -> x0, blocking collectives: 16.1 us -> none
    reduce_sum x12 -> x0, other arithmetic: 10.7 us -> none  [the longest x4 5.84 us: layer_norm(): mean_val = jnp.mean(residual, axis=-1, keepdims=True)]
    convert_element_type x5 -> x0, other arithmetic: 8.69 us -> none  [the longest x4 6.52 us: layer_norm(): (centered * lax.rsqrt(variance + 1e-05) * gain_vec + shift_vec).astype(jn...]
  transfers between devices with their start and end apart: 8 -> 0, of which waited for: 8 -> 0; matrix products, arithmetic and copies ran while one was open for 0% -> 0% of each run, Pallas kernels for 0% -> 0%
where the time goes in v3:
time: 515 us
  Pallas kernels  513 us (100%)
    pallas_call x1, Pallas kernels, device_fn(): pl.pallas_call(functools.partial(block_kernel, n), out_shape=jax.ShapeDty...  513 us

profile of v3, /device:TPU:21, one launch (start us, length us, event | category | flops | bytes accessed | tf_op | source)
XLA Modules:
  0.0 515.1 jit_solution(9729165066758950200)
XLA Ops:
  0.0 513.2 %shard_map.127 = bf16[64,4096]{1,0:T(8,128)(2,1)} custom-call(bf16[64,4096]{1,0:T(8,128)(2,1)} %bitcast.11, s32[1,64]{1,0:T(1,128)} %ids_ref.1, f32[2,4096]{1,0:T(2,128)} %g1_ref.1, f32[2,4096]{1,0:T(2,128)} %s1_ref.1, f32[2,4096]{1,0:T(2,128)} %ob_ref.1, f32[2,4096]{1,0:T(2,128)} %g2_ref.1, f32[2,4096]{1,0:T(2,128)} %s2_ref.1, f32[2,1024]{1,0:T(2,128)} %ub_ref.1, ...), custom_call_target="tpu_custom_call" | custom-call | tf_op jit(solution)/shard_map/pallas_call | solution.py:492
  513.2 1.9 copy.16

commit v4 on v3

--- a/solution.py
+++ b/solution.py
@@ -35,6 +35,7 @@
     units = wup.shape[1]
     tile = min(512, dim)
     utile = min(512, units)
+    wide = min(2048, dim)
 
     me = lax.axis_index("tp")
     core = lax.rem(me, 2)
@@ -102,11 +103,11 @@
             src_ref=ref, dst_ref=ref, send_sem=own_send.at[which, t], recv_sem=own_recv.at[which, t],
             device_id={"tp": sibling}, device_id_type=MESH)
 
-    def part_copy(piece):
-        slot, which = piece
+    def part_copy(slot, which, t):
+        rws = quarter_rows(which, t)
         return pltpu.make_async_remote_copy(
-            src_ref=part.at[slot, 1 - core, half_ds(which)], dst_ref=psib.at[slot, half_ds(which)],
-            send_sem=part_send.at[slot, which], recv_sem=part_recv.at[slot, which],
+            src_ref=part.at[slot, 1 - core, rws], dst_ref=psib.at[slot, rws],
+            send_sem=part_send.at[slot, which, t], recv_sem=part_recv.at[slot, which, t],
             device_id={"tp": sibling}, device_id_type=MESH)
 
     def rs_plan(direction, m):
@@ -126,27 +127,28 @@
             src_ref=src, dst_ref=ring.at[direction, m, t], send_sem=rs_send.at[direction, m, t], recv_sem=rs_recv.at[direction, m, t],
             device_id={"tp": target[direction]}, device_id_type=MESH)
 
-    def rs_step(m, need):
+    def sum_send(m, t, need):
         for direction in (RIGHT, LEFT):
             which, dest, before = rs_plan(direction, m)
-            need((dest, which))
+            need(dest, which, t)
+            if before is not None:
+                rs_copy(direction, before, t).wait_recv()
+            rws = quarter_rows(which, t)
+
+            def add(i):
+                cs = cols_at(i, tile)
+                total = part[dest, core, rws, cs].astype(F32) + psib[dest, rws, cs].astype(F32)
+                if before is None:
+                    fresh[direction, m, t, :, cs] = total
+                else:
+                    ring[direction, before, t, :, cs] = ring[direction, before, t, :, cs] + total
+
+            loop(dim // tile, add)
+            rs_copy(direction, m, t).start()
+
+    def rs_step(m, need):
         for t in range(2):
-            for direction in (RIGHT, LEFT):
-                which, dest, before = rs_plan(direction, m)
-                if before is not None:
-                    rs_copy(direction, before, t).wait_recv()
-                rws = quarter_rows(which, t)
-
-                def add(i):
-                    cs = cols_at(i, tile)
-                    total = part[dest, core, rws, cs].astype(F32) + psib[dest, rws, cs].astype(F32)
-                    if before is None:
-                        fresh[direction, m, t, :, cs] = total
-                    else:
-                        ring[direction, before, t, :, cs] = ring[direction, before, t, :, cs] + total
-
-                loop(dim // tile, add)
-                rs_copy(direction, m, t).start()
+            sum_send(m, t, need)
 
     def weight_copy(src, dst, index):
         return pltpu.make_async_copy(src, dst, w_sem.at[index])
@@ -195,6 +197,7 @@
                 total = total + ring[1 - which, steps - 3, t, :, cs] + ring[which, steps - 1, t, :, cs]
                 value = resid[rws, cs] + (total + bias_ref[pl.ds(layer, 1), cs])
                 resid[rws, cs] = value
+                out_ref[rws, cs] = value.astype(BF16)
                 out.append(acc[which] + value)
             return tuple(out)
 
@@ -216,17 +219,24 @@
                     rs_copy(direction, m, t).wait_send()
         for slot in range(chips):
             for which in range(2):
-                part_copy((slot, which)).wait_send()
+                for t in range(2):
+                    part_copy(slot, which, t).wait_send()
 
     def needs():
         seen = set()
 
-        def need(piece):
+        def need(*piece):
             if piece not in seen:
                 seen.add(piece)
-                part_copy(piece).wait_recv()
+                part_copy(*piece).wait_recv()
 
         return need
+
+    def need_all(need):
+        for slot in range(chips):
+            for which in range(2):
+                for t in range(2):
+                    need(slot, which, t)
 
     def gather_step(m, with_ids):
         for direction in (RIGHT, LEFT):
@@ -255,21 +265,31 @@
                 ag_copy(direction, m, with_ids).wait_send()
                 sib_copy(direction, m, with_ids).wait_send()
 
+    def piece_rows(piece):
+        slot, which, t = piece
+        return half_ds(which) if t is None else quarter_rows(which, t)
+
+    def piece_size(piece):
+        return rows if piece[2] is None else half_rows
+
     def load_rows(pieces):
-        return jnp.concatenate([hbuf[s, :, half_ds(w), pl.ds(0, dim)].reshape(rows, dim) for s, w in pieces], axis=0)
+        return jnp.concatenate([hbuf[p[0], :, piece_rows(p), pl.ds(0, dim)].reshape(piece_size(p), dim) for p in pieces], axis=0)
 
     def store_part(pieces, value, cs):
-        for i, (s, w) in enumerate(pieces):
-            part[s, :, half_ds(w), cs] = value[i * rows:(i + 1) * rows].reshape(2, half_rows, tile)
+        start = 0
+        for p in pieces:
+            size = piece_size(p)
+            part[p[0], :, piece_rows(p), cs] = value[start:start + size].reshape(2, size // 2, value.shape[1])
+            start += size
 
     def both(slot):
-        return [(slot, 0), (slot, 1)]
+        return [(slot, 0, None), (slot, 1, None)]
 
     minus, plus = slot_of(-(far - 1)), slot_of(far - 1)
     own = both(0)
     farthest = both(1)
-    leading = [(minus, 0), (plus, 1)]
-    trailing = [(minus, 1), (plus, 0)]
+    leading = [(minus, 0, None), (plus, 1, None)]
+    trailing = [(minus, 1, None), (plus, 0, None)]
 
     def near(p):
         return both(2 * p) + both(2 * p + 1)
@@ -278,8 +298,9 @@
     last_at = count - 1
 
     def send_parts(pieces):
-        for piece in pieces:
-            part_copy(piece).start()
+        for slot, which, t in pieces:
+            for u in range(2) if t is None else (t,):
+                part_copy(slot, which, u).start()
 
     def attention_half(layer):
         need = needs()
@@ -287,8 +308,8 @@
         def project(pieces, kinds=(0, 3)):
             def body(t):
                 value = jnp.dot(load_rows(pieces), wqkv[t], preferred_element_type=F32).astype(BF16)
-                for i, (s, w) in enumerate(pieces):
-                    qkv[t, s, :, half_ds(w)] = value[i * rows:(i + 1) * rows].reshape(2, half_rows, head)
+                for i, p in enumerate(pieces):
+                    qkv[t, p[0], :, piece_rows(p)] = value[i * rows:(i + 1) * rows].reshape(2, half_rows, head)
 
             lax.fori_loop(kinds[0], kinds[1], lambda t, carry: (body(t), carry)[1], 0)
 
@@ -298,21 +319,23 @@
             kids[:, cs] = jnp.concatenate(lines, axis=1)
 
         def column_ids(piece):
-            slot, which = piece
-            line = kids[0:1, pl.ds(slot * chip_rows, chip_rows)]
+            line = kids[0:1, pl.ds(piece[0] * chip_rows, chip_rows)]
             column = jnp.broadcast_to(line, (chip_rows, chip_rows)).T[:, 0:1]
-            return jnp.concatenate([column[c * rows + which * half_rows:c * rows + (which + 1) * half_rows] for c in range(2)], axis=0)
+            size = piece_size(piece) // 2
+            first = piece[1] * half_rows + (piece[2] or 0) * quarter
+            return jnp.concatenate([column[c * rows + first:c * rows + first + size] for c in range(2)], axis=0)
 
         def column_pos(piece):
-            slot, which = piece
-            i = lax.broadcasted_iota(jnp.int32, (rows, 1), 0)
-            i = i + jnp.where(i >= half_rows, rows - half_rows, 0)
-            return i + (which * half_rows + slot_chip(slot) * chip_rows)
+            size = piece_size(piece) // 2
+            first = piece[1] * half_rows + (piece[2] or 0) * quarter
+            i = lax.broadcasted_iota(jnp.int32, (2 * size, 1), 0)
+            i = i + jnp.where(i >= size, rows - size, 0)
+            return i + (first + slot_chip(piece[0]) * chip_rows)
 
         def attend(pieces):
             keys = qkv[1].reshape(chips * chip_rows, head)
             values = qkv[2].reshape(chips * chip_rows, head)
-            queries = jnp.concatenate([qkv[0, s, :, half_ds(w)].reshape(rows, head) for s, w in pieces], axis=0)
+            queries = jnp.concatenate([qkv[0, p[0], :, piece_rows(p)].reshape(piece_size(p), head) for p in pieces], axis=0)
             scores = lax.dot_general(queries, keys, (((1,), (1,)), ((), ())), preferred_element_type=F32) * (head ** -0.5)
             ids_col = jnp.concatenate([column_ids(piece) for piece in pieces], axis=0)
             pos_col = jnp.concatenate([column_pos(piece) for piece in pieces], axis=0)
@@ -324,10 +347,10 @@
             mixed = jnp.dot(probs, values, preferred_element_type=F32).astype(BF16)
 
             def proj(c):
-                cs = cols_at(c, tile)
+                cs = cols_at(c, wide)
                 store_part(pieces, jnp.dot(mixed, wout[:, cs], preferred_element_type=F32).astype(BF16), cs)
 
-            loop(dim // tile, proj)
+            loop(dim // wide, proj)
 
         weight_copy(wup_hbm.at[layer], wup, 2).start()
         weight_copy(wdown_hbm.at[layer], wdown, 3).start()
@@ -353,23 +376,26 @@
         sib_wait(last_at - 1, last_at, True)
         project(farthest, (1, 3))
         slot_ids(1)
-        attend(leading)
-        send_parts(leading)
+        for t in range(2):
+            quarters = [(slot, which, t) for slot, which, _ in leading]
+            attend(quarters)
+            send_parts(quarters)
+        rs_step(0, need)
         project(farthest, (0, 1))
-        rs_step(0, need)
         attend(farthest)
         send_parts(farthest)
         rs_step(1, need)
-        for pieces in [trailing] + [both(2 * p + i) for p in range(far - 2, 0, -1) for i in range(2)]:
-            attend(pieces)
-            send_parts(pieces)
         gather_end(True)
-        attend(own)
-        send_parts(own)
-        for m in range(2, steps):
-            rs_step(m, need)
-        for piece in own:
-            need(piece)
+        attend(trailing)
+        send_parts(trailing)
+        for p in range(far - 2, 0, -1):
+            for pieces in (both(2 * p), both(2 * p + 1)) + ((own,) if p == 1 else ()):
+                attend(pieces)
+                send_parts(pieces)
+            rs_step(2 * (far - 1 - p), need)
+            rs_step(2 * (far - 1 - p) + 1, need)
+        rs_step(steps - 1, need)
+        need_all(need)
 
     def mlp_half(layer):
         need = needs()
@@ -387,13 +413,14 @@
 
         def down(pieces):
             count_rows = rows * len(pieces)
+            step = min(wide, dim * 2 * rows // (2 * count_rows))
 
             def body(c):
-                cs = cols_at(c, tile)
+                cs = cols_at(c, step)
                 value = jnp.dot(hidden[pl.ds(0, count_rows), :], wdown[:, cs], preferred_element_type=F32).astype(BF16)
                 store_part(pieces, value, cs)
 
-            loop(dim // tile, body)
+            loop(dim // step, body)
 
         weight_copy(wup_hbm.at[layer], wup, 2).wait()
         weight_copy(wdown_hbm.at[layer], wdown, 3).wait()
@@ -411,15 +438,15 @@
             if m == 1:
                 down(own)
                 send_parts(own)
-            for p in range(1, far - 1):
+            for p in range(1, far - 2):
                 if m == 4 * p:
                     sib_wait(4 * p - 4, 4 * p - 1, False)
                     up(near(p))
-                if m == 4 * p + (0 if p == far - 2 else 1):
+                if m == 4 * p + 1:
                     down(near(p))
                     send_parts(near(p))
             if m == lead_at:
-                sib_wait(lead_at - 1, lead_at, False)
+                sib_wait(lead_at - 5, lead_at, False)
                 up(leading)
                 down(leading)
                 send_parts(leading)
@@ -428,13 +455,15 @@
         sib_wait(lead_at + 1, last_at, False)
         up(farthest + trailing)
         down(farthest + trailing)
+        send_parts(farthest + trailing)
+        rs_step(1, need)
         gather_end(False)
-        send_parts(farthest + trailing)
-        for m in range(1, steps):
+        up(near(far - 2))
+        down(near(far - 2))
+        send_parts(near(far - 2))
+        for m in range(2, steps):
             rs_step(m, need)
-        for slot in range(chips):
-            for piece in both(slot):
-                need(piece)
+        need_all(need)
 
     weight_copy(wqkv_hbm.at[0], wqkv, 0).start()
     weight_copy(wout_hbm.at[0], wout, 1).start()
@@ -466,7 +495,6 @@
         boundary(layer, db_ref, lax.rem(layer + 1, layers), g1_ref, s1_ref, True, layer + 1 < layers)
 
     loop(layers, layer_body)
-    loop(dim // tile, lambda i: out_ref.__setitem__((slice(None), cols_at(i, tile)), resid[:, cols_at(i, tile)].astype(BF16)))
 
 
 def solution(mesh):
@@ -510,7 +538,7 @@
                 pltpu.VMEM((8, chips * 2 * rows), jnp.int32),
                 pltpu.VMEM((8, chips * 2 * rows), F32),
                 dma((2, sends)), dma((2, sends)), dma((2, sends)), dma((2, sends)), dma((2, 2)), dma((2, 2)),
-                dma((chips, 2)), dma((chips, 2)), dma((2, steps, 2)), dma((2, steps, 2)), dma((4,)),
+                dma((chips, 2, 2)), dma((chips, 2, 2)), dma((2, steps, 2)), dma((2, steps, 2)), dma((4,)),
             ],
             compiler_params=pltpu.CompilerParams(collective_id=0, has_side_effects=True, vmem_limit_bytes=67043328),
         )(tokens.reshape(rows, dim), doc_ids, norm1_gain, norm1_shift, out_bias, norm2_gain, norm2_shift, up_bias, down_bias, wqkv, wout, up_weight, down_weight)

time: 515 us -> 504 us (0.979)
  Pallas kernels: 513 us -> 502 us
    pallas_call x1, Pallas kernels: 513 us -> 502 us  [device_fn(): pl.pallas_call(functools.partial(block_kernel, n), out_shape=jax.ShapeDty...]
where the time goes in v4:
time: 504 us
  Pallas kernels  502 us (100%)
    pallas_call x1, Pallas kernels, device_fn(): pl.pallas_call(functools.partial(block_kernel, n), out_shape=jax.ShapeDty...  502 us

profile of v4, /device:TPU:21, one launch (start us, length us, event | category | flops | bytes accessed | tf_op | source)
XLA Modules:
  0.0 503.6 jit_solution(8831581306984577331)
XLA Ops:
  0.0 501.7 %shard_map.127 = bf16[64,4096]{1,0:T(8,128)(2,1)} custom-call(bf16[64,4096]{1,0:T(8,128)(2,1)} %bitcast.11, s32[1,64]{1,0:T(1,128)} %ids_ref.1, f32[2,4096]{1,0:T(2,128)} %g1_ref.1, f32[2,4096]{1,0:T(2,128)} %s1_ref.1, f32[2,4096]{1,0:T(2,128)} %ob_ref.1, f32[2,4096]{1,0:T(2,128)} %g2_ref.1, f32[2,4096]{1,0:T(2,128)} %s2_ref.1, f32[2,1024]{1,0:T(2,128)} %ub_ref.1, ...), custom_call_target="tpu_custom_call" | custom-call | tf_op jit(solution)/shard_map/pallas_call | solution.py:520
  501.7 1.9 copy.16

commit v5 on v4

--- a/solution.py
+++ b/solution.py
@@ -22,8 +22,8 @@
 
 
 def block_kernel(n, tokens_ref, ids_ref, g1_ref, s1_ref, ob_ref, g2_ref, s2_ref, ub_ref, db_ref, wqkv_hbm, wout_hbm, wup_hbm, wdown_hbm,
-                 out_ref, hbuf, part, psib, ring, fresh, resid, wqkv, wout, wup, wdown, qkv, hidden, kpos, kids,
-                 ag_send, ag_recv, sib_send, sib_recv, own_send, own_recv, part_send, part_recv, rs_send, rs_recv, w_sem):
+                 resid, hbuf, part, psib, ring, fresh, lead, wqkv, wout, wup, wdown, qkv, hidden, kpos, kids,
+                 ag_send, ag_recv, sib_send, sib_recv, own_send, own_recv, part_send, part_recv, rs_send, rs_recv, lead_send, lead_recv, w_sem):
     chips = n // 2
     far = chips // 2
     steps = 2 * far - 1
@@ -43,6 +43,7 @@
     right, left = lax.rem(me + 2, n), lax.rem(me + n - 2, n)
     sibling = me + 1 - 2 * core
     target = (right, left)
+    crossed = (right + 1 - 2 * core, left + 1 - 2 * core)
 
     def slot_of(offset):
         if offset == 0:
@@ -122,16 +123,31 @@
 
     def rs_copy(direction, m, t):
         before = rs_plan(direction, m)[2]
-        src = fresh.at[direction, m, t] if before is None else ring.at[direction, before, t]
+        src = fresh.at[direction, t] if before is None else ring.at[direction, before, t]
         return pltpu.make_async_remote_copy(
             src_ref=src, dst_ref=ring.at[direction, m, t], send_sem=rs_send.at[direction, m, t], recv_sem=rs_recv.at[direction, m, t],
             device_id={"tp": target[direction]}, device_id_type=MESH)
+
+    def lead_copy(direction, t, cross):
+        which, dest, _ = rs_plan(direction, 0)
+        return pltpu.make_async_remote_copy(
+            src_ref=part.at[dest, 1 - core if cross else core, quarter_rows(which, t)], dst_ref=lead.at[direction, t, cross],
+            send_sem=lead_send.at[direction, t, cross], recv_sem=lead_recv.at[direction, t, cross],
+            device_id={"tp": (crossed if cross else target)[direction]}, device_id_type=MESH)
+
+    def lead_send_all(t):
+        for cross in (0, 1):
+            for direction in (RIGHT, LEFT):
+                lead_copy(direction, t, cross).start()
 
     def sum_send(m, t, need):
         for direction in (RIGHT, LEFT):
             which, dest, before = rs_plan(direction, m)
             need(dest, which, t)
-            if before is not None:
+            if before == 0:
+                for cross in (0, 1):
+                    lead_copy(direction, t, cross).wait_recv()
+            elif before is not None:
                 rs_copy(direction, before, t).wait_recv()
             rws = quarter_rows(which, t)
 
@@ -139,7 +155,10 @@
                 cs = cols_at(i, tile)
                 total = part[dest, core, rws, cs].astype(F32) + psib[dest, rws, cs].astype(F32)
                 if before is None:
-                    fresh[direction, m, t, :, cs] = total
+                    fresh[direction, t, :, cs] = total
+                elif before == 0:
+                    first = lead[direction, t, 0, :, cs].astype(F32) + lead[direction, t, 1, :, cs].astype(F32)
+                    ring[direction, 0, t, :, cs] = first + total
                 else:
                     ring[direction, before, t, :, cs] = ring[direction, before, t, :, cs] + total
 
@@ -197,7 +216,6 @@
                 total = total + ring[1 - which, steps - 3, t, :, cs] + ring[which, steps - 1, t, :, cs]
                 value = resid[rws, cs] + (total + bias_ref[pl.ds(layer, 1), cs])
                 resid[rws, cs] = value
-                out_ref[rws, cs] = value.astype(BF16)
                 out.append(acc[which] + value)
             return tuple(out)
 
@@ -213,14 +231,14 @@
                 @pl.when(more)
                 def _():
                     norm_send(t, sums, next_layer, gain_ref, shift_ref, with_ids)
-        for m in range(steps):
-            for direction in (RIGHT, LEFT):
-                for t in range(2):
+        for direction in (RIGHT, LEFT):
+            for t in range(2):
+                for cross in (0, 1):
+                    lead_copy(direction, t, cross).wait_send()
+                for m in range(1, steps):
                     rs_copy(direction, m, t).wait_send()
-        for slot in range(chips):
-            for which in range(2):
-                for t in range(2):
-                    part_copy(slot, which, t).wait_send()
+        for piece in exchanged:
+            part_copy(*piece).wait_send()
 
     def needs():
         seen = set()
@@ -233,10 +251,8 @@
         return need
 
     def need_all(need):
-        for slot in range(chips):
-            for which in range(2):
-                for t in range(2):
-                    need(slot, which, t)
+        for piece in exchanged:
+            need(*piece)
 
     def gather_step(m, with_ids):
         for direction in (RIGHT, LEFT):
@@ -290,6 +306,8 @@
     farthest = both(1)
     leading = [(minus, 0, None), (plus, 1, None)]
     trailing = [(minus, 1, None), (plus, 0, None)]
+
+    exchanged = [(slot, which, t) for slot in range(chips) for which in range(2) for t in range(2) if (slot, which, None) not in leading]
 
     def near(p):
         return both(2 * p) + both(2 * p + 1)
@@ -379,8 +397,7 @@
         for t in range(2):
             quarters = [(slot, which, t) for slot, which, _ in leading]
             attend(quarters)
-            send_parts(quarters)
-        rs_step(0, need)
+            lead_send_all(t)
         project(farthest, (0, 1))
         attend(farthest)
         send_parts(farthest)
@@ -449,8 +466,8 @@
                 sib_wait(lead_at - 5, lead_at, False)
                 up(leading)
                 down(leading)
-                send_parts(leading)
-        rs_step(0, need)
+                for t in range(2):
+                    lead_send_all(t)
         gather_step(last_at, False)
         sib_wait(lead_at + 1, last_at, False)
         up(farthest + trailing)
@@ -468,7 +485,7 @@
     weight_copy(wqkv_hbm.at[0], wqkv, 0).start()
     weight_copy(wout_hbm.at[0], wout, 1).start()
     barrier = pltpu.get_barrier_semaphore()
-    for device in (left, right, sibling):
+    for device in (left, right, sibling) + crossed:
         pl.semaphore_signal(barrier, inc=1, device_id={"tp": device}, device_id_type=MESH)
     hbuf[0, core, pl.ds(0, quarter), pl.ds(dim, ID_COLS)] = jnp.zeros((quarter, ID_COLS), BF16)
     hbuf[0, core, pl.ds(0, quarter), pl.ds(dim, rows)] = jnp.broadcast_to(ids_ref[...].astype(F32).astype(BF16), (quarter, rows))
@@ -486,7 +503,7 @@
 
         zero = jnp.zeros((quarter, tile), F32)
         sums = lax.fori_loop(0, dim // tile, widen, (zero, zero))
-        norm_send(t, sums, 0, g1_ref, s1_ref, True, (lambda: pl.semaphore_wait(barrier, 3)) if t == 0 else None)
+        norm_send(t, sums, 0, g1_ref, s1_ref, True, (lambda: pl.semaphore_wait(barrier, 5)) if t == 0 else None)
 
     def layer_body(layer):
         attention_half(layer)
@@ -519,7 +536,7 @@
         dma = pltpu.SemaphoreType.DMA
         result = pl.pallas_call(
             functools.partial(block_kernel, n),
-            out_shape=jax.ShapeDtypeStruct((rows, dim), BF16),
+            out_shape=jax.ShapeDtypeStruct((rows, dim), F32),
             in_specs=[vmem] * 9 + [hbm] * 4,
             out_specs=vmem,
             scratch_shapes=[
@@ -527,8 +544,8 @@
                 pltpu.VMEM((chips, 2, rows, dim), BF16),
                 pltpu.VMEM((chips, rows, dim), BF16),
                 pltpu.VMEM((2, steps, 2, rows // 4, dim), F32),
-                pltpu.VMEM((2, 2, 2, rows // 4, dim), F32),
-                pltpu.VMEM((rows, dim), F32),
+                pltpu.VMEM((2, 2, rows // 4, dim), F32),
+                pltpu.VMEM((2, 2, 2, rows // 4, dim), BF16),
                 pltpu.VMEM((3, dim, head), BF16),
                 pltpu.VMEM((head, dim), BF16),
                 pltpu.VMEM((dim, units), BF16),
@@ -538,10 +555,10 @@
                 pltpu.VMEM((8, chips * 2 * rows), jnp.int32),
                 pltpu.VMEM((8, chips * 2 * rows), F32),
                 dma((2, sends)), dma((2, sends)), dma((2, sends)), dma((2, sends)), dma((2, 2)), dma((2, 2)),
-                dma((chips, 2, 2)), dma((chips, 2, 2)), dma((2, steps, 2)), dma((2, steps, 2)), dma((4,)),
+                dma((chips, 2, 2)), dma((chips, 2, 2)), dma((2, steps, 2)), dma((2, steps, 2)), dma((2, 2, 2)), dma((2, 2, 2)), dma((4,)),
             ],
             compiler_params=pltpu.CompilerParams(collective_id=0, has_side_effects=True, vmem_limit_bytes=67043328),
         )(tokens.reshape(rows, dim), doc_ids, norm1_gain, norm1_shift, out_bias, norm2_gain, norm2_shift, up_bias, down_bias, wqkv, wout, up_weight, down_weight)
-        return result.reshape(batch, rows, dim)
+        return result.astype(BF16).reshape(batch, rows, dim)
 
     return jax.shard_map(device_fn, mesh=mesh, in_specs=in_specs, out_specs=row_spec, check_vma=False)

time: 504 us -> 502 us (level)
  no operation moved by 1% of the time
where the time goes in v5:
time: 502 us
  Pallas kernels  500 us (100%)
    pallas_call x1, Pallas kernels, device_fn(): pl.pallas_call(functools.partial(block_kernel, n), out_shape=jax.ShapeDty...  500 us

profile of v5, /device:TPU:21, one launch (start us, length us, event | category | flops | bytes accessed | tf_op | source)
XLA Modules:
  0.0 501.9 jit_solution(9713738149774513585)
XLA Ops:
  0.0 499.8 %shard_map.127 = f32[64,4096]{1,0:T(8,128)} custom-call(bf16[64,4096]{1,0:T(8,128)(2,1)} %bitcast.11, s32[1,64]{1,0:T(1,128)} %ids_ref.1, f32[2,4096]{1,0:T(2,128)} %g1_ref.1, f32[2,4096]{1,0:T(2,128)} %s1_ref.1, f32[2,4096]{1,0:T(2,128)} %ob_ref.1, f32[2,4096]{1,0:T(2,128)} %g2_ref.1, f32[2,4096]{1,0:T(2,128)} %s2_ref.1, f32[2,1024]{1,0:T(2,128)} %ub_ref.1, ...), custom_call_target="tpu_custom_call" | custom-call | tf_op jit(solution)/shard_map/pallas_call | solution.py:537
  499.8 2.1 convert_bitcast_fusion

commit v6 on v5

--- a/solution.py
+++ b/solution.py
@@ -22,7 +22,7 @@
 
 
 def block_kernel(n, tokens_ref, ids_ref, g1_ref, s1_ref, ob_ref, g2_ref, s2_ref, ub_ref, db_ref, wqkv_hbm, wout_hbm, wup_hbm, wdown_hbm,
-                 resid, hbuf, part, psib, ring, fresh, lead, wqkv, wout, wup, wdown, qkv, hidden, kpos, kids,
+                 out_ref, hbuf, part, psib, ring, fresh, lead, resid, wqkv, wout, wup, wdown, qkv, hidden, kpos, kids,
                  ag_send, ag_recv, sib_send, sib_recv, own_send, own_recv, part_send, part_recv, rs_send, rs_recv, lead_send, lead_recv, w_sem):
     chips = n // 2
     far = chips // 2
@@ -216,6 +216,7 @@
                 total = total + ring[1 - which, steps - 3, t, :, cs] + ring[which, steps - 1, t, :, cs]
                 value = resid[rws, cs] + (total + bias_ref[pl.ds(layer, 1), cs])
                 resid[rws, cs] = value
+                out_ref[rws, cs] = value.astype(BF16)
                 out.append(acc[which] + value)
             return tuple(out)
 
@@ -326,8 +327,11 @@
         def project(pieces, kinds=(0, 3)):
             def body(t):
                 value = jnp.dot(load_rows(pieces), wqkv[t], preferred_element_type=F32).astype(BF16)
-                for i, p in enumerate(pieces):
-                    qkv[t, p[0], :, piece_rows(p)] = value[i * rows:(i + 1) * rows].reshape(2, half_rows, head)
+                start = 0
+                for p in pieces:
+                    size = piece_size(p)
+                    qkv[t, p[0], :, piece_rows(p)] = value[start:start + size].reshape(2, size // 2, head)
+                    start += size
 
             lax.fori_loop(kinds[0], kinds[1], lambda t, carry: (body(t), carry)[1], 0)
 
@@ -391,9 +395,12 @@
                 project(leading + trailing)
                 slot_ids(minus)
                 slot_ids(plus)
-        sib_wait(last_at - 1, last_at, True)
-        project(farthest, (1, 3))
-        slot_ids(1)
+            if m >= last_at - 1:
+                t = m - last_at + 1
+                sib_wait(m, m, True)
+                project([(slot, which, t) for slot, which, _ in farthest], (1, 3))
+                if t == 0:
+                    slot_ids(1)
         for t in range(2):
             quarters = [(slot, which, t) for slot, which, _ in leading]
             attend(quarters)
@@ -536,7 +543,7 @@
         dma = pltpu.SemaphoreType.DMA
         result = pl.pallas_call(
             functools.partial(block_kernel, n),
-            out_shape=jax.ShapeDtypeStruct((rows, dim), F32),
+            out_shape=jax.ShapeDtypeStruct((rows, dim), BF16),
             in_specs=[vmem] * 9 + [hbm] * 4,
             out_specs=vmem,
             scratch_shapes=[
@@ -546,6 +553,7 @@
                 pltpu.VMEM((2, steps, 2, rows // 4, dim), F32),
                 pltpu.VMEM((2, 2, rows // 4, dim), F32),
                 pltpu.VMEM((2, 2, 2, rows // 4, dim), BF16),
+                pltpu.VMEM((rows, dim), F32),
                 pltpu.VMEM((3, dim, head), BF16),
                 pltpu.VMEM((head, dim), BF16),
                 pltpu.VMEM((dim, units), BF16),
@@ -559,6 +567,6 @@
             ],
             compiler_params=pltpu.CompilerParams(collective_id=0, has_side_effects=True, vmem_limit_bytes=67043328),
         )(tokens.reshape(rows, dim), doc_ids, norm1_gain, norm1_shift, out_bias, norm2_gain, norm2_shift, up_bias, down_bias, wqkv, wout, up_weight, down_weight)
-        return result.astype(BF16).reshape(batch, rows, dim)
+        return result.reshape(batch, rows, dim)
 
     return jax.shard_map(device_fn, mesh=mesh, in_specs=in_specs, out_specs=row_spec, check_vma=False)

time: 502 us -> 503 us (level)
  no operation moved by 1% of the time
where the time goes in v6:
time: 503 us; the launch traced here: 502 us
  Pallas kernels  501 us (100%)
    pallas_call x1, Pallas kernels, device_fn(): pl.pallas_call(functools.partial(block_kernel, n), out_shape=jax.ShapeDty...  501 us

profile of v6, /device:TPU:21, one launch (start us, length us, event | category | flops | bytes accessed | tf_op | source)
XLA Modules:
  0.0 502.4 jit_solution(5452974572955906430)
XLA Ops:
  0.0 500.6 %shard_map.127 = bf16[64,4096]{1,0:T(8,128)(2,1)} custom-call(bf16[64,4096]{1,0:T(8,128)(2,1)} %bitcast.11, s32[1,64]{1,0:T(1,128)} %ids_ref.1, f32[2,4096]{1,0:T(2,128)} %g1_ref.1, f32[2,4096]{1,0:T(2,128)} %s1_ref.1, f32[2,4096]{1,0:T(2,128)} %ob_ref.1, f32[2,4096]{1,0:T(2,128)} %g2_ref.1, f32[2,4096]{1,0:T(2,128)} %s2_ref.1, f32[2,1024]{1,0:T(2,128)} %ub_ref.1, ...), custom_call_target="tpu_custom_call" | custom-call | tf_op jit(solution)/shard_map/pallas_call | solution.py:544
  500.6 1.9 copy.16

commit v7 on v6

--- a/solution.py
+++ b/solution.py
@@ -395,12 +395,11 @@
                 project(leading + trailing)
                 slot_ids(minus)
                 slot_ids(plus)
-            if m >= last_at - 1:
-                t = m - last_at + 1
-                sib_wait(m, m, True)
-                project([(slot, which, t) for slot, which, _ in farthest], (1, 3))
-                if t == 0:
-                    slot_ids(1)
+        for t in range(2):
+            sib_wait(last_at - 1 + t, last_at - 1 + t, True)
+            if t == 0:
+                slot_ids(1)
+            project([(slot, which, t) for slot, which, _ in farthest], (1, 3))
         for t in range(2):
             quarters = [(slot, which, t) for slot, which, _ in leading]
             attend(quarters)

time: 503 us -> 501 us (level)
  no operation moved by 1% of the time
where the time goes in v7:
time: 501 us
  Pallas kernels  499 us (100%)
    pallas_call x1, Pallas kernels, device_fn(): pl.pallas_call(functools.partial(block_kernel, n), out_shape=jax.ShapeDty...  499 us

profile of v7, /device:TPU:21, one launch (start us, length us, event | category | flops | bytes accessed | tf_op | source)
XLA Modules:
  0.0 500.7 jit_solution(301045811346598328)
XLA Ops:
  0.0 498.8 %shard_map.127 = bf16[64,4096]{1,0:T(8,128)(2,1)} custom-call(bf16[64,4096]{1,0:T(8,128)(2,1)} %bitcast.11, s32[1,64]{1,0:T(1,128)} %ids_ref.1, f32[2,4096]{1,0:T(2,128)} %g1_ref.1, f32[2,4096]{1,0:T(2,128)} %s1_ref.1, f32[2,4096]{1,0:T(2,128)} %ob_ref.1, f32[2,4096]{1,0:T(2,128)} %g2_ref.1, f32[2,4096]{1,0:T(2,128)} %s2_ref.1, f32[2,1024]{1,0:T(2,128)} %ub_ref.1, ...), custom_call_target="tpu_custom_call" | custom-call | tf_op jit(solution)/shard_map/pallas_call | solution.py:543
  498.8 1.9 copy.16

commit v8 on v7

--- a/solution.py
+++ b/solution.py
@@ -476,14 +476,17 @@
                     lead_send_all(t)
         gather_step(last_at, False)
         sib_wait(lead_at + 1, last_at, False)
-        up(farthest + trailing)
-        down(farthest + trailing)
-        send_parts(farthest + trailing)
+        up(farthest)
+        down(farthest)
+        send_parts(farthest)
         rs_step(1, need)
-        gather_end(False)
         up(near(far - 2))
         down(near(far - 2))
         send_parts(near(far - 2))
+        gather_end(False)
+        up(trailing)
+        down(trailing)
+        send_parts(trailing)
         for m in range(2, steps):
             rs_step(m, need)
         need_all(need)

time: 501 us -> 501 us (level)
  no operation moved by 1% of the time
where the time goes in v8:
time: 501 us
  Pallas kernels  499 us (100%)
    pallas_call x1, Pallas kernels, device_fn(): pl.pallas_call(functools.partial(block_kernel, n), out_shape=jax.ShapeDty...  499 us

profile of v8, /device:TPU:21, one launch (start us, length us, event | category | flops | bytes accessed | tf_op | source)
XLA Modules:
  0.0 501.1 jit_solution(16821796155381838720)
XLA Ops:
  0.0 499.3 %shard_map.127 = bf16[64,4096]{1,0:T(8,128)(2,1)} custom-call(bf16[64,4096]{1,0:T(8,128)(2,1)} %bitcast.11, s32[1,64]{1,0:T(1,128)} %ids_ref.1, f32[2,4096]{1,0:T(2,128)} %g1_ref.1, f32[2,4096]{1,0:T(2,128)} %s1_ref.1, f32[2,4096]{1,0:T(2,128)} %ob_ref.1, f32[2,4096]{1,0:T(2,128)} %g2_ref.1, f32[2,4096]{1,0:T(2,128)} %s2_ref.1, f32[2,1024]{1,0:T(2,128)} %ub_ref.1, ...), custom_call_target="tpu_custom_call" | custom-call | tf_op jit(solution)/shard_map/pallas_call | solution.py:546
  499.3 1.9 copy.16
